TPU v7x, 512 devices: a whole 4x8x8 slice. The times are simulated.
512 devices in a mesh: leaf: 128 (over y, z, core), sub: 4 (over x).
Axes of the slice: x: 4, y: 8, z: 8, core: 2. Of those that a mesh axis runs over, the one named last changes fastest.
Arguments:
- vectors: bfloat16 [64, 131072], P('sub', 'leaf'), may hold values from -6 to 6
- near_blocks: bfloat16 [512, 9, 256, 256], P(('leaf', 'sub')), may hold values from -0.125 to 0.125
- near_cols: int32 [512, 9], P(('leaf', 'sub')), may hold values from 0 to 511, as said below
- near_mask: int32 [512, 9], P(('leaf', 'sub')), may hold values from 0 to 1, as said below
- leaf_basis: bfloat16 [512, 32, 256], P('leaf'), may hold values from -0.375 to 0.375
- transfer: bfloat16 [768, 32, 32], P('leaf'), may hold values from -1 to 1
- coupling: bfloat16 [896, 27, 32, 32], P('leaf'), may hold values from -0.3125 to 0.3125
- far_targets: int32 [896, 27], P('leaf'), may hold values from 0 to 895, as said below
- far_mask: int32 [896, 27], P('leaf'), may hold values from 0 to 1
Outputs:
- result: bfloat16 [64, 131072], P('sub', 'leaf')
Inputs may be any that keep to these rules, and one draw needn't show every extreme that they name: `near_cols`: row i names 9 leaves; its first entry is leaf i; every entry is a leaf of the subtree of leaf i or of the subtree just before or after it; the entries marked live are distinct. `near_mask`: the first entry of each row is 1. `far_targets`: entry (c, k) names a cluster on the same level as cluster c, in any subtree. The 189 entries of one subtree's rows, masked ones included, name clusters of any one subtree at most 2 times; in every draw some subtree is named exactly 2 times, by live entries, from every subtree.
All inputs are finite; a program needn't handle non-finite values.
Results may differ from a plain program's by a relative error of at most 0.0065.
Values may be sent and summed in bfloat16 or wider, within the bound.
A program may use at most 64 MiB of HBM per device.

v0:
```python
import jax
import jax.numpy as jnp
from jax import lax
from jax.sharding import PartitionSpec as P


def with_halo(cells, sides, width):
    for axis, dim in sides:
        count = lax.axis_size(axis)
        ends = count - 1
        head = lax.slice_in_dim(cells, 0, width, axis=dim)
        tail = lax.slice_in_dim(cells, cells.shape[dim] - width, cells.shape[dim], axis=dim)
        cells = jnp.concatenate(
            [
                lax.ppermute(tail, axis, [(i, (i + 1) % count) for i in range(ends)]),
                cells,
                lax.ppermute(head, axis, [((i + 1) % count, i) for i in range(ends)]),
            ],
            axis=dim,
        )
    return cells


def near_field(window, blocks, columns, alive_mask, first_leaf, leaf_size):
    row_count = window.shape[0]
    pieces = window.reshape(row_count, window.shape[1] // leaf_size, leaf_size)
    relative = (columns - first_leaf).reshape(-1)
    taken = jnp.take(pieces, relative, axis=1)
    taken = taken.reshape(row_count, columns.shape[0], columns.shape[1], leaf_size)
    taken = taken * alive_mask.astype(jnp.bfloat16)[None, :, :, None]
    product = jnp.einsum("vjkp,jkpq->vjq", taken, blocks, preferred_element_type=jnp.float32)
    return product.reshape(row_count, columns.shape[0] * leaf_size)


def pack_slots(values, owners, places, peer_count, capacity):
    highest = lax.Precision.HIGHEST
    peer_ids = jnp.arange(peer_count, dtype=jnp.int32)
    onehot = (owners[:, None] == peer_ids[None, :]).astype(jnp.int32)
    rank_within = jnp.sum(onehot * (jnp.cumsum(onehot, axis=0) - 1), axis=1)
    slot_of = owners * capacity + rank_within
    slot_ids = jnp.arange(peer_count * capacity, dtype=jnp.int32)
    select = slot_ids[:, None] == slot_of[None, :]
    send_values = jnp.dot(select.astype(jnp.float32), values, precision=highest)
    send_places = jnp.sum(jnp.where(select, places[None, :], 0), axis=1)
    return (send_values, send_places)


def sum_slots(got_values, got_places, clusters):
    cluster_ids = jnp.arange(clusters, dtype=jnp.int32)
    hits = (got_places[None, :] == cluster_ids[:, None]).astype(jnp.float32)
    return jnp.dot(hits, got_values, precision=lax.Precision.HIGHEST)


def local(
    vectors,
    near_blocks,
    near_cols,
    near_mask,
    leaf_basis,
    transfer,
    coupling,
    far_targets,
    far_mask,
):
    highest = lax.Precision.HIGHEST
    leaf_size = leaf_basis.shape[2]
    subtree = leaf_basis.shape[0]
    clusters = coupling.shape[0]
    far_count = coupling.shape[1]
    rank_size = coupling.shape[2]
    own_vecs = vectors.shape[0]
    peer_count = lax.axis_size("leaf")
    tree_index = lax.axis_index("leaf")
    window_first = (tree_index - 1) * subtree
    padded = with_halo(vectors, (("leaf", 1),), subtree * leaf_size)
    window = lax.all_gather(padded, "sub", axis=0, tiled=True)
    near_part = near_field(window, near_blocks, near_cols, near_mask, window_first, leaf_size)
    near_total = lax.all_to_all(
        near_part.astype(jnp.bfloat16), "sub", split_axis=0, concat_axis=1, tiled=True
    ).astype(near_part.dtype)
    sizes_all = []
    level_size = subtree
    while level_size >= 1:
        sizes_all.append(level_size)
        level_size = level_size // 2
    starts_all = [sum(sizes_all[:number]) for number in range(len(sizes_all))]
    maps_all = transfer.astype(jnp.float32)
    leaf_pieces = vectors.reshape(own_vecs, subtree, leaf_size)
    coeffs = jnp.einsum("vsp,srp->svr", leaf_pieces, leaf_basis, preferred_element_type=jnp.float32)
    hats = [coeffs]
    for level_no in range(len(sizes_all) - 1):
        level_size = sizes_all[level_no]
        level_start = starts_all[level_no]
        child = hats[-1].reshape(level_size // 2, 2, own_vecs, rank_size)
        level_maps = maps_all[level_start : level_start + level_size].reshape(
            level_size // 2, 2, rank_size, rank_size
        )
        hats.append(jnp.einsum("pcvr,pcrq->pvq", child, level_maps, precision=highest))
    all_hats = jnp.concatenate(hats, axis=0)
    terms = jnp.einsum("cvr,ckrq->ckvq", all_hats, coupling.astype(jnp.float32), precision=highest)
    terms = terms * far_mask.astype(jnp.float32)[:, :, None, None]
    terms = terms.reshape(clusters * far_count, own_vecs * rank_size)
    owners = (far_targets // clusters).reshape(-1)
    places = (far_targets % clusters).reshape(-1)
    capacity = max(2, (4 * clusters * far_count + 3 * peer_count - 1) // (3 * peer_count))
    send_values, send_places = pack_slots(terms, owners, places, peer_count, capacity)
    got_values, got_places = (
        lax.all_to_all(
            send_values.astype(jnp.bfloat16), "leaf", split_axis=0, concat_axis=0, tiled=True
        ).astype(send_values.dtype),
        lax.all_to_all(send_places, "leaf", split_axis=0, concat_axis=0, tiled=True),
    )
    incoming = sum_slots(got_values, got_places, clusters)
    incoming = incoming.reshape(clusters, own_vecs, rank_size)
    downward = [
        incoming[starts_all[number] : starts_all[number] + sizes_all[number]]
        for number in range(len(sizes_all))
    ]
    for level_no in range(len(sizes_all) - 2, -1, -1):
        level_size = sizes_all[level_no]
        level_start = starts_all[level_no]
        level_maps = maps_all[level_start : level_start + level_size].reshape(
            level_size // 2, 2, rank_size, rank_size
        )
        pushed = jnp.einsum("pvq,pcrq->pcvr", downward[level_no + 1], level_maps, precision=highest)
        downward[level_no] = downward[level_no] + pushed.reshape(level_size, own_vecs, rank_size)
    far_out = jnp.einsum(
        "svr,srp->vsp", downward[0], leaf_basis.astype(jnp.float32), precision=highest
    )
    far_out = far_out.reshape(own_vecs, subtree * leaf_size)
    return (near_total + far_out).astype(jnp.bfloat16)


def solution(mesh):
    return jax.shard_map(
        local,
        mesh=mesh,
        in_specs=(
            P("sub", "leaf"),
            P(("leaf", "sub"), None, None, None),
            P(("leaf", "sub"), None),
            P(("leaf", "sub"), None),
            P("leaf", None, None),
            P("leaf", None, None),
            P("leaf", None, None, None),
            P("leaf", None),
            P("leaf", None),
        ),
        out_specs=P("sub", "leaf"),
        check_vma=False,
    )
```

profile of v0, /device:TPU:8, one launch (start us, length us, event | category | flops | bytes accessed | tf_op | source)
XLA Modules:
  0.0 80.0 jit_solution(838098052362511047)
XLA Ops:
  0.0 10.4 %collective-permute-start.1 = (bf16[16,1024]{1,0:T(8,128)(2,1)}, bf16[16,1024]{1,0:T(8,128)(2,1)}, u32[]{:S(2)}, u32[]{:S(2)}) collective-permute-start(bf16[16,1024]{1,0:T(8,128)(2,1)} %param.9), channel_id=1, source_target_pairs={{4,0},{8,4},{12,8},{16,12},{20,16},{24,20},{28,24},{32,28},{36,32}... | collective-permute-start | bytes 98312 | tf_op jit(solution)/shard_map/ppermute | solution.py:17
  10.4 1.9 %collective-permute-start = (bf16[16,1024]{1,0:T(8,128)(2,1)}, bf16[16,1024]{1,0:T(8,128)(2,1)}, u32[]{:S(2)}, u32[]{:S(2)}) collective-permute-start(bf16[16,1024]{1,0:T(8,128)(2,1)} %param.9), channel_id=1, source_target_pairs={{0,4},{4,8},{8,12},{12,16},{16,20},{20,24},{24,28},{28,32},{32,36}... | collective-permute-start | bytes 98312 | tf_op jit(solution)/shard_map/ppermute | solution.py:15
  12.3 0.7 add_select_fusion
  13.9 0.8 all_to_all.23
  14.7 12.7 %all-to-all-start.1 = ((s32[128,2,1]{1,2,0:T(1,128)}), s32[128,2,1]{1,2,0:T(1,128)}, u32[]{:S(2)}, u32[]{:S(2)}) async-start(s32[128,2,1]{1,2,0:T(1,128)} %bitcast.15), calls=%async_computation.1 | async-start | bytes 131072 | tf_op jit(solution)/shard_map/all_to_all | solution.py:111
  27.4 1.2 %fusion.35 = s32[9]{0:T(128)} fusion(s32[1,9]{1,0:T(1,128)} %param.11, s32[]{:T(128)S(6)} %mul.40), kind=kLoop, calls=%fused_computation.61 | loop fusion | flops 36 | bytes 76 | tf_op jit(solution)/shard_map/jit(_take)/jit(_where)/select_n | solution.py:28
  28.7 1.2 %compare_and_fusion = pred[9]{0:T(512)(128)(4,1)} fusion(s32[1,9]{1,0:T(1,128)} %param.11, s32[]{:T(128)S(6)} %mul.40), kind=kLoop, calls=%fused_computation.58 | loop fusion | flops 63 | bytes 49 | tf_op jit(solution)/shard_map/jit(_take)/and | solution.py:28
  29.9 0.7 convert_element_type.54
  30.5 0.8 slice.36
  31.3 1.0 %fusion.27 = f32[4,16,32]{2,1,0:T(8,128)S(1)} fusion(bf16[4,32,256]{2,1,0:T(8,128)(2,1)} %param.13, bf16[2,4,8,256]{3,2,1,0:T(8,128)(2,1)} %bitcast.110), kind=kOutput, calls=%fused_computation.40 | convolution fusion | flops 1048576 | bytes 106496 | tf_op jit(solution)/shard_map/vsp,srp->svr/dot_general | solution.py:89
  32.5 0.9 %convolution_bitcast_fusion.2 = f32[1,16,32]{2,1,0:T(8,128)S(1)} fusion(f32[2,16,32]{2,1,0:T(8,128)S(1)} %convolution_bitcast_fusion.1, bf16[6,32,32]{2,1,0:T(8,128)(2,1)} %param.14), kind=kOutput, calls=%fused_computation.14 | convolution fusion | flops 393216 | bytes 22528 | tf_op jit(solution)/shard_map/pcvr,pcrq->pvq/dot_general | solution.py:98
  33.4 0.8 %multiply_bitcast_fusion = f32[7,27,16,32]{3,2,1,0:T(8,128)S(1)} fusion(bf16[7,27,32,32]{3,2,1,0:T(8,128)(2,1)S(1)} %copy-done, f32[7,27]{1,0:T(8,128)S(1)} %convert_element_type.54, f32[1,16,32]{2,1,0:T(8,128)S(1)} %convolution_bitcast_fusion.2, f32[2,16,32]{2,1,0:T(8,128)S(1)} %convolution_bitcast_fusion.1, f32[4,16,32]{2,1,0:T(8,128)S(1)} %fusion.27), kind=kOutput, calls=%fused_computation.1 | convolution fusion | flops 37262848 | bytes 789236 | tf_op jit(solution)/shard_map/cvr,ckrq->ckvq/dot_general | solution.py:100
  34.9 1.2 %convolution_convert_fusion = bf16[256,512]{1,0:T(8,128)(2,1)S(1)} fusion(f32[189,512]{1,0:T(8,128)S(1)} %reshape.145, s32[189]{0:T(256)} %copy-done.4), kind=kOutput, calls=%fused_computation.2 | convolution fusion | flops 297450752 | bytes 649972 | tf_op jit(solution)/shard_map/dot_general | solution.py:43
  36.7 0.7 pad_clamp_fusion
  37.4 0.8 all_to_all.25
  38.2 14.3 %all-to-all-start.2 = ((bf16[128,2,512]{2,1,0:T(2,128)(2,1)}), bf16[128,2,512]{2,1,0:T(2,128)(2,1)}, u32[]{:S(2)}, u32[]{:S(2)}) async-start(bf16[128,2,512]{2,1,0:T(2,128)(2,1)} %all_to_all.25), calls=%async_computation.2 | async-start | bytes 524288 | tf_op jit(solution)/shard_map/all_to_all | solution.py:108
  53.0 1.7 %reduce.7 = s32[128,2]{1,0:T(8,128)S(1)} reduce(s32[128,2,1]{1,2,0:T(1,128)} %all-to-all-done.1, s32[]{:T(128)} %broadcast.99), dimensions={2}, to_apply=%all_to_all.24.reduce_sub_computation.3 | reduce | bytes 2052 | tf_op jit(solution)/shard_map/all_to_all | solution.py:111
  54.8 0.8 pad_maximum_fusion
  55.6 12.9 %all_gather.3 = bf16[64,3072]{1,0:T(8,128)(2,1)S(1)} all-gather(bf16[16,3072]{1,0:T(8,128)(2,1)S(1)} %pad_maximum_fusion), channel_id=1, replica_groups=mesh['leaf'=128,'sub'=4] {'sub'}, dimensions={0}, use_global_device_ids=true | all-gather | bytes 491520 | tf_op jit(solution)/shard_map/all_gather | solution.py:76
  69.1 1.0 %fusion.5 = bf16[64,256]{1,0:T(8,128)(2,1)} fusion(bf16[1,9,256,256]{3,2,1,0:T(8,128)(2,1)S(1)} %copy-done.1, bf16[9,64,256]{2,1,0:T(8,128)(2,1)S(1)} %gather_fusion, pred[9]{0:T(512)(128)(4,1)S(1)} %copy-done.5, bf16[9]{0:T(256)(128)(2,1)S(1)} %convert_bitcast_fusion), kind=kOutput, calls=%fused_computation.7 | convolution fusion | flops 75808768 | bytes 1507355 | tf_op jit(solution)/shard_map/vjkp,jkpq->vjq/dot_general | solution.py:31
  70.1 3.7 %all-to-all-start = ((bf16[4,16,256]{2,1,0:T(8,128)(2,1)}), bf16[4,16,256]{2,1,0:T(8,128)(2,1)S(1)}, u32[]{:S(2)}, u32[]{:S(2)}) async-start(bf16[4,16,256]{2,1,0:T(8,128)(2,1)} %bitcast.10), calls=%async_computation | async-start | bytes 65536 | tf_op jit(solution)/shard_map/all_to_all | solution.py:78
  73.8 1.1 %all_to_all.27 = bf16[256,512]{1,0:T(8,128)(2,1)S(1)} reshape(bf16[128,2,512]{2,1,0:T(2,128)(2,1)} %all-to-all-done.2) | data formatting | bytes 524288 | tf_op jit(solution)/shard_map/all_to_all | solution.py:108
  75.3 0.9 %fusion.11 = f32[2,16,32,1]{2,1,3,0:T(8,128)S(1)} fusion(f32[2,16,32]{2,1,0:T(8,128)S(1)} %slice.41, f32[16,32,1]{1,0,2:T(8,128)S(1)} %reshape.162, bf16[6,32,32]{2,1,0:T(8,128)(2,1)} %param.14), kind=kOutput, calls=%fused_computation.12 | convolution fusion | flops 394240 | bytes 26624 | tf_op jit(solution)/shard_map/pvq,pcrq->pcvr/dot_general | solution.py:125
  76.5 2.8 %all-to-all-done = bf16[4,16,256]{2,1,0:T(8,128)(2,1)S(1)} async-done(((bf16[4,16,256]{2,1,0:T(8,128)(2,1)}), bf16[4,16,256]{2,1,0:T(8,128)(2,1)S(1)}, u32[]{:S(2)}, u32[]{:S(2)}) %all-to-all-start) | async-done | bytes 32800 | tf_op jit(solution)/shard_map/all_to_all | solution.py:78
  (48 shorter events, 5.0 us)
Async XLA Ops:
  0.0 33.4 %copy-start = (bf16[7,27,32,32]{3,2,1,0:T(8,128)(2,1)S(1)}, bf16[7,27,32,32]{3,2,1,0:T(8,128)(2,1)}, u32[]{:S(2)}) copy-start(bf16[7,27,32,32]{3,2,1,0:T(8,128)(2,1)} %param.15) | copy-start | bytes 1161220
  0.0 54.8 %collective-permute-start.1 = (bf16[16,1024]{1,0:T(8,128)(2,1)}, bf16[16,1024]{1,0:T(8,128)(2,1)}, u32[]{:S(2)}, u32[]{:S(2)}) collective-permute-start(bf16[16,1024]{1,0:T(8,128)(2,1)} %param.9), channel_id=1, source_target_pairs={{4,0},{8,4},{12,8},{16,12},{20,16},{24,20},{28,24},{32,28},{36,32}... | collective-permute-start | bytes 98312 | tf_op jit(solution)/shard_map/ppermute | solution.py:17
  10.4 44.4 %collective-permute-start = (bf16[16,1024]{1,0:T(8,128)(2,1)}, bf16[16,1024]{1,0:T(8,128)(2,1)}, u32[]{:S(2)}, u32[]{:S(2)}) collective-permute-start(bf16[16,1024]{1,0:T(8,128)(2,1)} %param.9), channel_id=1, source_target_pairs={{0,4},{4,8},{8,12},{12,16},{16,20},{20,24},{24,28},{28,32},{32,36}... | collective-permute-start | bytes 98312 | tf_op jit(solution)/shard_map/ppermute | solution.py:15
  13.7 16.2 %copy-start.4 = (s32[189]{0:T(256)}, s32[189]{0:T(256)S(1)}, u32[]{:S(2)}) copy-start(s32[189]{0:T(256)S(1)} %multiply_add_fusion) | copy-start | bytes 2272
  14.7 23.5 %all-to-all-start.1 = ((s32[128,2,1]{1,2,0:T(1,128)}), s32[128,2,1]{1,2,0:T(1,128)}, u32[]{:S(2)}, u32[]{:S(2)}) async-start(s32[128,2,1]{1,2,0:T(1,128)} %bitcast.15), calls=%async_computation.1 | async-start | bytes 131072 | tf_op jit(solution)/shard_map/all_to_all | solution.py:111
  34.3 20.6 %copy-start.3 = (bf16[16,1024]{1,0:T(8,128)(2,1)S(1)}, bf16[16,1024]{1,0:T(8,128)(2,1)}, u32[]{:S(2)}) copy-start(bf16[16,1024]{1,0:T(8,128)(2,1)} %param.9) | copy-start | bytes 98308
  38.2 30.9 %copy-start.1 = (bf16[1,9,256,256]{3,2,1,0:T(8,128)(2,1)S(1)}, bf16[1,9,256,256]{3,2,1,0:T(8,128)(2,1)}, u32[]{:S(2)}) copy-start(bf16[1,9,256,256]{3,2,1,0:T(8,128)(2,1)} %param.10) | copy-start | bytes 3538948
  38.2 30.9 %copy-start.5 = (pred[9]{0:T(512)(128)(4,1)S(1)}, pred[9]{0:T(512)(128)(4,1)}, u32[]{:S(2)}) copy-start(pred[9]{0:T(512)(128)(4,1)} %compare_and_fusion) | copy-start | bytes 31
  38.2 31.9 %all-to-all-start.2 = ((bf16[128,2,512]{2,1,0:T(2,128)(2,1)}), bf16[128,2,512]{2,1,0:T(2,128)(2,1)}, u32[]{:S(2)}, u32[]{:S(2)}) async-start(bf16[128,2,512]{2,1,0:T(2,128)(2,1)} %all_to_all.25), calls=%async_computation.2 | async-start | bytes 524288 | tf_op jit(solution)/shard_map/all_to_all | solution.py:108
  69.1 10.1 %copy-start.2 = (bf16[4,32,256]{2,1,0:T(8,128)(2,1)S(1)}, bf16[4,32,256]{2,1,0:T(8,128)(2,1)}, u32[]{:S(2)}) copy-start(bf16[4,32,256]{2,1,0:T(8,128)(2,1)} %param.13) | copy-start | bytes 196612
  70.1 9.1 %all-to-all-start = ((bf16[4,16,256]{2,1,0:T(8,128)(2,1)}), bf16[4,16,256]{2,1,0:T(8,128)(2,1)S(1)}, u32[]{:S(2)}, u32[]{:S(2)}) async-start(bf16[4,16,256]{2,1,0:T(8,128)(2,1)} %bitcast.10), calls=%async_computation | async-start | bytes 65536 | tf_op jit(solution)/shard_map/all_to_all | solution.py:78
where the time goes:
time: 80.9 us; the launch traced here: 80 us
  starting transfers between devices  43.1 us (53%)
  blocking collectives  12.9 us (16%)
  other arithmetic  8.26 us (10%)
  matrix products  6.51 us (8%)
  local copies, waits for them, and re-layouts  6.29 us (8%)
  waiting for transfers between devices  2.8 us (3%)
    all_to_all x1, starting transfers between devices, local(): lax.all_to_all(send_values.astype(jnp.bfloat16), 'leaf', split_axis=0, co...  14.3 us
    all_gather x1, blocking collectives, local(): window = lax.all_gather(padded, 'sub', axis=0, tiled=True)  12.9 us
    all_to_all x1, starting transfers between devices, local(): lax.all_to_all(send_places, 'leaf', split_axis=0, concat_axis=0, tiled=True)  12.7 us
    ppermute x1, starting transfers between devices, with_halo(): lax.ppermute(head, axis, [((i + 1) % count, i) for i in range(ends)])  10.4 us
    all_to_all x1, starting transfers between devices, local(): lax.all_to_all(near_part.astype(jnp.bfloat16), 'sub', split_axis=0, conca...  3.68 us
    all_to_all x1, waiting for transfers between devices, local(): lax.all_to_all(near_part.astype(jnp.bfloat16), 'sub', split_axis=0, conca...  2.79 us
    ppermute x1, starting transfers between devices, with_halo(): lax.ppermute(tail, axis, [(i, (i + 1) % count) for i in range(ends)])  1.92 us
    all_to_all x2, local copies, waits for them, and re-layouts, local(): lax.all_to_all(send_values.astype(jnp.bfloat16), 'leaf', split_axis=0, co...  1.84 us
  transfers between devices with their start and end apart: 5, of which 1 were waited for; matrix products, arithmetic and copies ran while one was open for 22% of the time, Pallas kernels for 0%

commit v1 on v0

v1 whole, which is shorter than its diff:
```python
import jax
import jax.numpy as jnp
from jax import lax
from jax.experimental import pallas as pl
from jax.experimental.pallas import tpu as pltpu
from jax.sharding import PartitionSpec as P

MESH = pl.DeviceIdType.MESH
F32 = jnp.float32
BF16 = jnp.bfloat16
GROUPS = 8
MEMBERS = 16
LEAVES = 128
SUBS = 4


def iota(shape, dim):
    return lax.broadcasted_iota(jnp.int32, shape, dim)


def fiota(shape, dim):
    return iota(shape, dim).astype(F32)


def peer(group, member):
    return (member // 2) * 16 + group * 2 + member % 2


def slot_choice(targets, alive, wide):
    wide[...] = jnp.zeros((2, 8, 128), F32)
    wide[0, 0:7, 0:27] = targets.astype(F32)
    wide[1, 0:7, 0:27] = alive.astype(F32)
    flat = []
    for which in range(2):
        rows = wide[which]
        rows = rows + pltpu.roll(rows, 64, 1)
        rows = rows + pltpu.roll(rows, 32, 1)
        tiles = []
        for tile in range(2):
            own = iota((8, 128), 0) == tile * 4 + iota((8, 128), 1) // 32
            tiles.append(jnp.sum(jnp.where(own, rows, 0.0), axis=0, keepdims=True))
        flat.append(jnp.concatenate(tiles, axis=1))
    named, live = flat
    lane = iota((1, 256), 1)
    valid = (lane % 32 < 27) & (lane < 224)
    tree = jnp.floor((named + 0.5) * (1.0 / 7.0))
    place = named - 7.0 * tree
    along_y = jnp.floor((tree + 0.5) * (1.0 / 16.0))
    half = jnp.floor((tree + 0.5) * 0.5)
    order = (half - 8.0 * along_y) * 16.0 + along_y * 2.0 + (tree - 2.0 * half)
    order = jnp.where(valid, order, -1.0)
    hit = fiota((128, 256), 0) == order
    hits = jnp.where(hit, 1.0, 0.0).astype(BF16)
    before = jnp.where(iota((256, 256), 0) < iota((256, 256), 1), 1.0, 0.0).astype(BF16)
    earlier = jnp.dot(hits, before, preferred_element_type=F32)
    kept = jnp.where(hit, live, 0.0)
    first = jnp.where(earlier < 0.5, kept, 0.0)
    second = jnp.where(earlier > 0.5, kept, 0.0)
    place_first = jnp.sum(first * place, axis=1, keepdims=True)
    place_second = jnp.sum(second * place, axis=1, keepdims=True)
    column = iota((128, 128), 1)
    places = jnp.where(column < 64, place_first, place_second) * 8.0 + (column % 8).astype(F32)
    return jnp.concatenate([first, second], axis=0).astype(BF16), places


def kernel(
    vec,
    blocks,
    near_cols,
    near_mask,
    basis,
    transfer,
    coupling,
    far_targets,
    far_mask,
    out,
    v_own,
    v_blk,
    v_basis,
    v_map,
    v_coup,
    v_tgt,
    v_msk,
    wide,
    terms,
    packed,
    slabs,
    send_v,
    send_p,
    recv_v,
    recv_p,
    window,
    near_out,
    near_in,
    down,
    acc,
    s_cols,
    s_mask,
    load_sem,
    send_sem,
    recv_v_sem,
    recv_p_sem,
    near_sem,
):
    me = lax.axis_index("leaf")
    sub = lax.axis_index("sub")
    group = (me // 2) % GROUPS
    member = (me // 16) * 2 + me % 2

    loads = [
        pltpu.make_async_copy(far_targets, v_tgt, load_sem.at[0]),
        pltpu.make_async_copy(far_mask, v_msk, load_sem.at[1]),
        pltpu.make_async_copy(basis, v_basis, load_sem.at[2]),
        pltpu.make_async_copy(transfer, v_map, load_sem.at[3]),
        pltpu.make_async_copy(coupling, v_coup.at[:, pl.ds(0, 27)], load_sem.at[4]),
        pltpu.make_async_copy(near_cols, s_cols, load_sem.at[5]),
        pltpu.make_async_copy(near_mask, s_mask, load_sem.at[6]),
        pltpu.make_async_copy(blocks.at[0], v_blk, load_sem.at[7]),
    ] + [
        pltpu.make_async_copy(vec.at[:, pl.ds(leaf * 256, 256)], v_own.at[leaf], load_sem.at[8 + leaf])
        for leaf in range(4)
    ]
    for copy in loads:
        copy.start()

    barrier = pltpu.get_barrier_semaphore()

    def greet_later(n, carry):
        pl.semaphore_signal(
            barrier,
            inc=1,
            device_id={"leaf": peer(GROUPS - 1 - n // MEMBERS, n % MEMBERS)},
            device_id_type=MESH,
        )
        return carry

    lax.fori_loop(0, (GROUPS - 1 - group) * MEMBERS, greet_later, 0)

    def greet_own(n, carry):
        pl.semaphore_signal(
            barrier,
            inc=1,
            device_id={"leaf": peer(group, (member + n) % MEMBERS)},
            device_id_type=MESH,
        )
        return carry

    lax.fori_loop(1, MEMBERS, greet_own, 0)
    near_peers = [(shift, turn) for shift in (-1, 0, 1) for turn in range(SUBS) if (shift, turn) != (0, 0)]
    for shift, turn in near_peers:
        pl.semaphore_signal(
            barrier,
            inc=1,
            device_id={"leaf": (me + shift + LEAVES) % LEAVES, "sub": (sub + turn) % SUBS},
            device_id_type=MESH,
        )

    v_coup[:, 27:32] = jnp.zeros((7, 5, 32, 32), BF16)

    loads[0].wait()
    loads[1].wait()
    choice, places = slot_choice(v_tgt[...], v_msk[...], wide)
    send_p[...] = places.reshape(128, 1, 128)

    pl.semaphore_wait(barrier, group * MEMBERS + (MEMBERS - 1) + len(near_peers))

    def send_place(to_group, to_member):
        pltpu.make_async_remote_copy(
            src_ref=send_p.at[to_group * MEMBERS + to_member],
            dst_ref=recv_p.at[group, member],
            send_sem=send_sem.at[0],
            recv_sem=recv_p_sem.at[group],
            device_id={"leaf": peer(to_group, to_member)},
            device_id_type=MESH,
        ).start()

    def send_value(to_group, to_member):
        pltpu.make_async_remote_copy(
            src_ref=send_v.at[to_group * MEMBERS + to_member],
            dst_ref=recv_v.at[group, member],
            send_sem=send_sem.at[1],
            recv_sem=recv_v_sem.at[group],
            device_id={"leaf": peer(to_group, to_member)},
            device_id_type=MESH,
        ).start()

    def to_earlier(send):
        def one(n, carry):
            send(n // MEMBERS, n % MEMBERS)
            return carry

        lax.fori_loop(0, group * MEMBERS, one, 0)

        def own(n, carry):
            send(group, (member + n) % MEMBERS)
            return carry

        lax.fori_loop(1, MEMBERS, own, 0)

    to_earlier(send_place)

    for leaf in range(4):
        loads[8 + leaf].wait()
    loads[2].wait()
    loads[3].wait()
    across = (((1,), (1,)), ((), ()))
    up = [
        lax.dot_general(v_own[leaf], v_basis[leaf], across, preferred_element_type=F32).astype(BF16)
        for leaf in range(4)
    ]
    for pair in range(3):
        up.append(
            (
                jnp.dot(up[2 * pair], v_map[2 * pair], preferred_element_type=F32)
                + jnp.dot(up[2 * pair + 1], v_map[2 * pair + 1], preferred_element_type=F32)
            ).astype(BF16)
        )
    loads[4].wait()
    same = iota((128, 256), 0) // 16 == iota((128, 256), 1) // 32
    for c in range(7):
        left = jnp.concatenate([up[c]] * 8, axis=1)
        left = jnp.concatenate([left] * 8, axis=0)
        left = jnp.where(same, left, jnp.zeros_like(left))
        right = jnp.concatenate(
            [v_coup[c, 8 * g : 8 * g + 8].reshape(256, 32) for g in range(4)], axis=1
        )
        terms[c * 128 : (c + 1) * 128, :] = jnp.dot(left, right, preferred_element_type=F32)
    lane_group = iota((8, 128), 1) // 32
    for c in range(7):
        for tile in range(4):
            rows = [
                terms[pl.ds(c * 128 + (lg % 2) * 8 + 2 * tile + lg // 2, 8, stride=16), :]
                for lg in range(4)
            ]
            turned = []
            for delta in range(4):
                mixed = rows[delta]
                for g in range(1, 4):
                    mixed = jnp.where(lane_group == g, rows[(g + delta) % 4], mixed)
                turned.append(pltpu.roll(mixed, 32 * delta, 1) if delta else mixed)
            done = []
            for g in range(4):
                mixed = turned[(0 - g) % 4]
                for lg in range(1, 4):
                    mixed = jnp.where(lane_group == lg, turned[(lg - g) % 4], mixed)
                done.append(mixed)
            packed[c * 32 : c * 32 + 32, tile * 128 : (tile + 1) * 128] = jnp.concatenate(
                done, axis=0
            ).astype(BF16)
    packed[224:256, :] = jnp.zeros((32, 512), BF16)
    chosen = jnp.dot(choice, packed[...], preferred_element_type=F32)
    low_half = iota((8, 128), 1) < 64
    for block in range(16):
        for tile in range(4):
            a = chosen[block * 8 : block * 8 + 8, tile * 128 : (tile + 1) * 128]
            b = chosen[128 + block * 8 : 136 + block * 8, tile * 128 : (tile + 1) * 128]
            even = jnp.where(low_half, a, pltpu.roll(b, 64, 1))
            odd = jnp.where(low_half, pltpu.roll(a, 64, 1), b)
            slabs[pl.ds(block * 64 + 2 * tile, 8, stride=8), :] = even
            slabs[pl.ds(block * 64 + 2 * tile + 1, 8, stride=8), :] = odd
    send_v[...] = slabs[...].reshape(128, 8, 128).astype(BF16)

    to_earlier(send_value)

    for shift, turn in near_peers:
        pltpu.make_async_remote_copy(
            src_ref=v_own,
            dst_ref=window.at[pl.ds((1 - shift) * 4, 4), pl.ds(sub * 16, 16), :],
            send_sem=near_sem.at[0],
            recv_sem=near_sem.at[1],
            device_id={"leaf": (me + shift + LEAVES) % LEAVES, "sub": (sub + turn) % SUBS},
            device_id_type=MESH,
        ).start()
    window[4:8, pl.ds(pl.multiple_of(sub * 16, 16), 16), :] = v_own[...]
    mine = group * MEMBERS + member
    recv_v[group, member] = send_v[mine]
    recv_p[group, member] = send_p[mine]

    down[...] = jnp.zeros((256, 1024), BF16)
    first_dims = (((0,), (0,)), ((), ()))
    for leaf in range(4):
        at = slice(leaf * 256, (leaf + 1) * 256)
        down[leaf * 32 : leaf * 32 + 32, at] = v_basis[leaf]
        once = lax.dot_general(v_map[leaf], v_basis[leaf], first_dims, preferred_element_type=F32).astype(BF16)
        parent = 4 + leaf // 2
        down[parent * 32 : parent * 32 + 32, at] = once
        twice = lax.dot_general(v_map[parent], once, first_dims, preferred_element_type=F32)
        down[192:224, at] = twice.astype(BF16)

    loads[5].wait()
    loads[6].wait()
    loads[7].wait()
    pltpu.make_async_copy(window.at[pl.ds(0, 11)], window.at[pl.ds(0, 11)], near_sem.at[1]).wait()
    near = jnp.zeros((64, 256), F32)
    for k in range(9):
        source = window[jnp.clip(s_cols[0, k] - (me - 1) * 4, 0, 11)]
        keep = s_mask[0, k].astype(F32)
        near = near + keep * jnp.dot(source, v_blk[k], preferred_element_type=F32)
    near_out[...] = near.reshape(4, 16, 256).astype(BF16)
    for turn in range(1, SUBS):
        pltpu.make_async_remote_copy(
            src_ref=near_out.at[(sub + turn) % SUBS],
            dst_ref=near_in.at[sub],
            send_sem=near_sem.at[2],
            recv_sem=near_sem.at[3],
            device_id={"sub": (sub + turn) % SUBS},
            device_id_type=MESH,
        ).start()
    near_in[sub] = near_out[sub]

    acc[...] = jnp.zeros((64, 128), F32)

    def take(from_group):
        got = recv_p[from_group].reshape(16, 128)
        swapped = pltpu.roll(got, 64, 1)
        low = iota((16, 128), 1) < 64
        own = iota((16, 128), 0) == iota((16, 128), 1) // 8
        values = recv_v[from_group].astype(F32).reshape(128, 128).astype(BF16)
        sums = []
        for each in (jnp.where(low, got, swapped), jnp.where(low, swapped, got)):
            row = jnp.sum(jnp.where(own, each, 0.0), axis=0, keepdims=True)
            weight = jnp.where(fiota((64, 128), 0) == row, 1.0, 0.0).astype(BF16)
            sums.append(jnp.dot(weight, values, preferred_element_type=F32))
        acc[...] += jnp.where(iota((64, 128), 1) < 64, sums[0], sums[1])

    def wait_group(ref, sem, from_group, count):
        pltpu.make_async_copy(
            ref.at[from_group, pl.ds(0, count)], ref.at[from_group, pl.ds(0, count)], sem.at[from_group]
        ).wait()

    def later(n, carry):
        from_group = group + 1 + n
        wait_group(recv_p, recv_p_sem, from_group, MEMBERS)

        def answer(m, inner):
            send_place(from_group, m)
            send_value(from_group, m)
            return inner

        lax.fori_loop(0, MEMBERS, answer, 0)
        wait_group(recv_v, recv_v_sem, from_group, MEMBERS)
        take(from_group)
        return carry

    lax.fori_loop(0, GROUPS - 1 - group, later, 0)
    wait_group(recv_p, recv_p_sem, group, MEMBERS - 1)
    wait_group(recv_v, recv_v_sem, group, MEMBERS - 1)
    take(group)

    def earlier(n, carry):
        wait_group(recv_p, recv_p_sem, n, MEMBERS)
        wait_group(recv_v, recv_v_sem, n, MEMBERS)
        take(n)
        return carry

    lax.fori_loop(0, group, earlier, 0)

    total = acc[...]
    total = total + pltpu.roll(total, 64, 1)
    lane_group = iota((8, 128), 1) // 32
    halves = []
    for high in range(2):
        tiles = []
        for tile in range(2):
            mixed = jnp.zeros((8, 128), F32)
            for lg in range(4):
                c = tile * 4 + lg
                if c < 7:
                    part = total[c * 8 : c * 8 + 8, :]
                    turn = (lg * 32 - high * 32) % 128
                    part = pltpu.roll(part, turn, 1) if turn else part
                    mixed = jnp.where(lane_group == lg, part, mixed)
            tiles.append(mixed)
        halves.append(jnp.concatenate(tiles, axis=1))
    incoming = jnp.concatenate(halves, axis=0).astype(BF16)
    far = jnp.dot(incoming, down[...], preferred_element_type=F32)
    pltpu.make_async_copy(near_in.at[pl.ds(0, 3)], near_in.at[pl.ds(0, 3)], near_sem.at[3]).wait()
    for leaf in range(4):
        at = slice(leaf * 256, (leaf + 1) * 256)
        out[:, at] = (near_in[leaf].astype(F32) + far[:, at]).astype(BF16)

    pltpu.make_async_copy(send_p.at[pl.ds(0, 127)], send_p.at[pl.ds(0, 127)], send_sem.at[0]).wait()
    pltpu.make_async_copy(send_v.at[pl.ds(0, 127)], send_v.at[pl.ds(0, 127)], send_sem.at[1]).wait()
    pltpu.make_async_copy(window.at[pl.ds(0, 11)], window.at[pl.ds(0, 11)], near_sem.at[0]).wait()
    pltpu.make_async_copy(near_out.at[pl.ds(0, 3)], near_out.at[pl.ds(0, 3)], near_sem.at[2]).wait()


def local(*args):
    any_space = pl.BlockSpec(memory_space=pl.ANY)
    dma = pltpu.SemaphoreType.DMA
    vmem = pltpu.VMEM
    return pl.pallas_call(
        kernel,
        out_shape=jax.ShapeDtypeStruct((16, 1024), BF16),
        in_specs=[any_space] * 9,
        out_specs=pl.BlockSpec(memory_space=pltpu.VMEM),
        scratch_shapes=[
            vmem((4, 16, 256), BF16),
            vmem((9, 256, 256), BF16),
            vmem((4, 32, 256), BF16),
            vmem((6, 32, 32), BF16),
            vmem((7, 32, 32, 32), BF16),
            vmem((7, 27), jnp.int32),
            vmem((7, 27), jnp.int32),
            vmem((2, 8, 128), F32),
            vmem((896, 128), F32),
            vmem((256, 512), BF16),
            vmem((1024, 128), F32),
            vmem((128, 8, 128), BF16),
            vmem((128, 1, 128), F32),
            vmem((8, 16, 8, 128), BF16),
            vmem((8, 16, 1, 128), F32),
            vmem((12, 64, 256), BF16),
            vmem((4, 16, 256), BF16),
            vmem((4, 16, 256), BF16),
            vmem((256, 1024), BF16),
            vmem((64, 128), F32),
            pltpu.SMEM((1, 9), jnp.int32),
            pltpu.SMEM((1, 9), jnp.int32),
            dma((12,)),
            dma((2,)),
            dma((8,)),
            dma((8,)),
            dma((4,)),
        ],
        compiler_params=pltpu.CompilerParams(collective_id=0, has_side_effects=True),
    )(*args)


def solution(mesh):
    return jax.shard_map(
        local,
        mesh=mesh,
        in_specs=(
            P("sub", "leaf"),
            P(("leaf", "sub"), None, None, None),
            P(("leaf", "sub"), None),
            P(("leaf", "sub"), None),
            P("leaf", None, None),
            P("leaf", None, None),
            P("leaf", None, None, None),
            P("leaf", None),
            P("leaf", None),
        ),
        out_specs=P("sub", "leaf"),
        check_vma=False,
    )
```

time: 80.9 us -> 38.1 us (0.47)
  starting transfers between devices: 43.1 us -> 0 us
  Pallas kernels: 0 us -> 36.6 us
  blocking collectives: 12.9 us -> 0 us
  other arithmetic: 8.26 us -> 0 us
  matrix products: 6.51 us -> 0 us
  local copies, waits for them, and re-layouts: 6.29 us -> 1.38 us
  waiting for transfers between devices: 2.8 us -> 0 us
    pallas_call x0 -> x1, Pallas kernels: none -> 36.6 us  [local(): pl.pallas_call(kernel, out_shape=jax.ShapeDtypeStruct((16, 1024), BF16),...]
    all_to_all x3 -> x0, starting transfers between devices: 30.7 us -> none  [the longest x1 14.3 us: local(): lax.all_to_all(send_values.astype(jnp.bfloat16), 'leaf', split_axis=0, co...]
    all_gather x1 -> x0, blocking collectives: 12.9 us -> none  [local(): window = lax.all_gather(padded, 'sub', axis=0, tiled=True)]
    ppermute x2 -> x0, starting transfers between devices: 12.3 us -> none  [the longest x1 10.4 us: with_halo(): lax.ppermute(head, axis, [((i + 1) % count, i) for i in range(ends)])]
    dot_general x10 -> x0, matrix products: 6.51 us -> none  [the longest x1 1.17 us: pack_slots(): send_values = jnp.dot(select.astype(jnp.float32), values, precision=highest)]
    all_to_all x4 -> x0, local copies, waits for them, and re-layouts: 3.12 us -> none  [the longest x2 1.84 us: local(): lax.all_to_all(send_values.astype(jnp.bfloat16), 'leaf', split_axis=0, co...]
    all_to_all x3 -> x0, waiting for transfers between devices: 2.8 us -> none  [the longest x1 2.79 us: local(): lax.all_to_all(near_part.astype(jnp.bfloat16), 'sub', split_axis=0, conca...]
    select_n x2 -> x0, other arithmetic: 1.95 us -> none  [the longest x1 1.25 us: near_field(): taken = jnp.take(pieces, relative, axis=1)]
  transfers between devices with their start and end apart: 5 -> 0, of which waited for: 1 -> 0; matrix products, arithmetic and copies ran while one was open for 22% -> 0% of each run, Pallas kernels for 0% -> 0%
where the time goes in v1:
time: 38.1 us; the launch traced here: 38 us
  Pallas kernels  36.6 us (96%)
  local copies, waits for them, and re-layouts  1.38 us (4%)
    pallas_call x1, Pallas kernels, local(): pl.pallas_call(kernel, out_shape=jax.ShapeDtypeStruct((16, 1024), BF16),...  36.6 us
    unnamed x1, local copies, waits for them, and re-layouts  1.38 us

profile of v1, /device:TPU:8, one launch (start us, length us, event | category | flops | bytes accessed | tf_op | source)
XLA Modules:
  0.0 38.0 jit_solution(12992101538828225618)
XLA Ops:
  0.0 36.6 %shard_map.91 = bf16[16,1024]{1,0:T(8,128)(2,1)} custom-call(bf16[16,1024]{1,0:T(8,128)(2,1)} %vec.1, bf16[1,9,256,256]{3,2,1,0:T(8,128)(2,1)} %blocks.1, s32[1,9]{1,0:T(1,128)} %near_cols.1, s32[1,9]{1,0:T(1,128)} %near_mask.1, bf16[4,32,256]{2,1,0:T(8,128)(2,1)} %basis.1, bf16[6,32,32]{2,1,0:T(8,128)(2,1)} %transfer.1, bf16[7,27,32,32]{3,2,1,0:T(8,128)(2,1)} %coupling.1, ...), custom_call_target="tpu_custom_call" | custom-call | tf_op jit(solution)/shard_map/pallas_call | solution.py:392
  36.6 1.4 %copy.11 = bf16[16,1024]{1,0:T(8,128)(2,1)} copy(bf16[16,1024]{1,0:T(8,128)(2,1)} %shard_map.91) | data formatting | bytes 65536

commit v2 on v1

v2 whole, which is shorter than its diff:
```python
import jax
import jax.numpy as jnp
from jax import lax
from jax.experimental import pallas as pl
from jax.experimental.pallas import tpu as pltpu
from jax.sharding import PartitionSpec as P

MESH = pl.DeviceIdType.MESH
F32 = jnp.float32
BF16 = jnp.bfloat16
GROUPS = 16
MEMBERS = 8
QUAD = 4
QUADS = GROUPS // QUAD
LEAVES = 128
SUBS = 4


def iota(shape, dim):
    return lax.broadcasted_iota(jnp.int32, shape, dim)


def fiota(shape, dim):
    return iota(shape, dim).astype(F32)


def peer(group, member):
    along_y = ((group // 4) % 2) * 4 + member // 2
    return along_y * 16 + ((group // 8) * 4 + group % 4) * 2 + member % 2


def wide_dot(left, right):
    high = left.astype(BF16)
    low = (left - high.astype(F32)).astype(BF16)
    rows = left.shape[0]
    both = jnp.dot(jnp.concatenate([high, low], axis=0), right, preferred_element_type=F32)
    return both[:rows] + both[rows:]


def slot_choice(targets, alive, wide):
    wide[...] = jnp.zeros((2, 8, 128), F32)
    wide[0, 0:7, 0:27] = targets.astype(F32)
    wide[1, 0:7, 0:27] = alive.astype(F32)
    flat = []
    for which in range(2):
        rows = wide[which]
        rows = rows + pltpu.roll(rows, 64, 1)
        rows = rows + pltpu.roll(rows, 32, 1)
        tiles = []
        for tile in range(2):
            own = iota((8, 128), 0) == tile * 4 + iota((8, 128), 1) // 32
            tiles.append(jnp.sum(jnp.where(own, rows, 0.0), axis=0, keepdims=True))
        flat.append(jnp.concatenate(tiles, axis=1))
    named, live = flat
    lane = iota((1, 256), 1)
    valid = (lane % 32 < 27) & (lane < 224)
    tree = jnp.floor((named + 0.5) * (1.0 / 7.0))
    place = named - 7.0 * tree
    along_y = jnp.floor((tree + 0.5) * (1.0 / 16.0))
    half = jnp.floor((tree + 0.5) * 0.5)
    along_z = half - 8.0 * along_y
    half_y = jnp.floor((along_y + 0.5) * 0.25)
    half_z = jnp.floor((along_z + 0.5) * 0.25)
    order = (4.0 * half_z + 4.0 * half_y + along_z) * 8.0 + (along_y - 4.0 * half_y) * 2.0 + (tree - 2.0 * half)
    order = jnp.where(valid, order, -1.0)
    hit = fiota((128, 256), 0) == order
    hits = jnp.where(hit, 1.0, 0.0).astype(BF16)
    before = jnp.where(iota((256, 256), 0) < iota((256, 256), 1), 1.0, 0.0).astype(BF16)
    earlier = jnp.dot(hits, before, preferred_element_type=F32)
    kept = jnp.where(hit, live, 0.0)
    first = jnp.where(earlier < 0.5, kept, 0.0)
    second = jnp.where(earlier > 0.5, kept, 0.0)
    place_first = jnp.sum(first * place, axis=1, keepdims=True)
    place_second = jnp.sum(second * place, axis=1, keepdims=True)
    places = jnp.where(iota((128, 32), 1) < 16, place_first, place_second)
    return jnp.concatenate([first, second], axis=0).astype(BF16), places


def kernel(
    vec,
    blocks,
    near_cols,
    near_mask,
    basis,
    transfer,
    coupling,
    far_targets,
    far_mask,
    out,
    v_own,
    v_blk,
    v_basis,
    v_map,
    v_coup,
    v_tgt,
    v_msk,
    wide,
    terms,
    packed,
    slabs,
    send_v,
    send_p,
    recv_v,
    recv_p,
    window,
    near_out,
    near_in,
    down,
    acc,
    s_cols,
    s_mask,
    load_sem,
    send_sem,
    recv_v_sem,
    recv_p_sem,
    near_sem,
):
    me = lax.axis_index("leaf")
    sub = lax.axis_index("sub")
    group = ((me // 8) % 2) * 8 + (me // 64) * 4 + (me // 2) % 4
    member = ((me // 16) % 4) * 2 + me % 2

    loads = [
        pltpu.make_async_copy(far_targets, v_tgt, load_sem.at[0]),
        pltpu.make_async_copy(far_mask, v_msk, load_sem.at[1]),
        pltpu.make_async_copy(basis, v_basis, load_sem.at[2]),
        pltpu.make_async_copy(transfer, v_map, load_sem.at[3]),
        pltpu.make_async_copy(coupling, v_coup.at[:, pl.ds(0, 27)], load_sem.at[4]),
        pltpu.make_async_copy(near_cols, s_cols, load_sem.at[5]),
        pltpu.make_async_copy(near_mask, s_mask, load_sem.at[6]),
        pltpu.make_async_copy(blocks.at[0], v_blk, load_sem.at[7]),
    ] + [
        pltpu.make_async_copy(vec.at[:, pl.ds(leaf * 256, 256)], v_own.at[leaf], load_sem.at[8 + leaf])
        for leaf in range(4)
    ]
    for copy in loads:
        copy.start()

    barrier = pltpu.get_barrier_semaphore()

    def greet(to_group, to_member):
        pl.semaphore_signal(
            barrier, inc=1, device_id={"leaf": peer(to_group, to_member)}, device_id_type=MESH
        )

    for n in range(1, MEMBERS):
        greet(group, (member + n) % MEMBERS)

    def has(shift):
        return (me + shift >= 0) & (me + shift < LEAVES)

    across_sub = [{"sub": (sub + turn) % SUBS} for turn in range(1, SUBS)]

    first_z = me % 16 == 0
    last_z = me % 16 == 15
    across_after = [{"leaf": me + 1, "sub": (sub + turn) % SUBS} for turn in range(1, SUBS)]
    across_before = [{"leaf": me - 1, "sub": (sub + turn) % SUBS} for turn in range(1, SUBS)]

    def near_peers(shift):
        return across_sub if shift == 0 else [{"leaf": me + shift}]

    for shift in (-1, 0, 1):

        @pl.when(has(shift))
        def _():
            for target in near_peers(shift):
                pl.semaphore_signal(barrier, inc=1, device_id=target, device_id_type=MESH)

    @pl.when(first_z & has(-1))
    def _():
        for target in across_before:
            pl.semaphore_signal(barrier, inc=1, device_id=target, device_id_type=MESH)

    def greet_later(n, carry):
        for m in range(MEMBERS):
            greet(n, m)
        return carry

    lax.fori_loop(group + 1, GROUPS, greet_later, 0)

    v_coup[:, 27:32] = jnp.zeros((7, 5, 32, 32), BF16)

    loads[0].wait()
    loads[1].wait()
    choice, places = slot_choice(v_tgt[...], v_msk[...], wide)
    send_p[...] = places.reshape(128, 1, 32)

    for leaf in range(4):
        loads[8 + leaf].wait()
    loads[2].wait()
    loads[3].wait()
    across = (((1,), (1,)), ((), ()))
    up = [
        lax.dot_general(v_own[leaf], v_basis[leaf], across, preferred_element_type=F32)
        for leaf in range(4)
    ]
    for pair in range(3):
        up.append(wide_dot(up[2 * pair], v_map[2 * pair]) + wide_dot(up[2 * pair + 1], v_map[2 * pair + 1]))
    loads[4].wait()
    same = iota((128, 256), 0) // 16 == iota((128, 256), 1) // 32
    for c in range(7):
        left = jnp.concatenate([up[c].astype(BF16)] * 8, axis=1)
        left = jnp.concatenate([left] * 8, axis=0)
        left = jnp.where(same, left, jnp.zeros_like(left))
        right = jnp.concatenate(
            [v_coup[c, 8 * g : 8 * g + 8].reshape(256, 32) for g in range(4)], axis=1
        )
        terms[c * 128 : (c + 1) * 128, :] = jnp.dot(left, right, preferred_element_type=F32)
    lane_group = iota((8, 128), 1) // 32
    for c in range(7):
        for tile in range(4):
            rows = [
                terms[pl.ds(c * 128 + (lg % 2) * 8 + 2 * tile + lg // 2, 8, stride=16), :]
                for lg in range(4)
            ]
            turned = []
            for delta in range(4):
                mixed = rows[delta]
                for g in range(1, 4):
                    mixed = jnp.where(lane_group == g, rows[(g + delta) % 4], mixed)
                turned.append(pltpu.roll(mixed, 32 * delta, 1) if delta else mixed)
            done = []
            for g in range(4):
                mixed = turned[(0 - g) % 4]
                for lg in range(1, 4):
                    mixed = jnp.where(lane_group == lg, turned[(lg - g) % 4], mixed)
                done.append(mixed)
            packed[c * 32 : c * 32 + 32, tile * 128 : (tile + 1) * 128] = jnp.concatenate(
                done, axis=0
            ).astype(BF16)
    packed[224:256, :] = jnp.zeros((32, 512), BF16)
    chosen = jnp.dot(choice, packed[...], preferred_element_type=F32)
    low_half = iota((8, 128), 1) < 64
    for block in range(16):
        for tile in range(4):
            a = chosen[block * 8 : block * 8 + 8, tile * 128 : (tile + 1) * 128]
            b = chosen[128 + block * 8 : 136 + block * 8, tile * 128 : (tile + 1) * 128]
            even = jnp.where(low_half, a, pltpu.roll(b, 64, 1))
            odd = jnp.where(low_half, pltpu.roll(a, 64, 1), b)
            slabs[pl.ds(block * 64 + 2 * tile, 8, stride=8), :] = even
            slabs[pl.ds(block * 64 + 2 * tile + 1, 8, stride=8), :] = odd
    send_v[...] = slabs[...].reshape(128, 8, 128).astype(BF16)

    near_count = 3 + has(-1).astype(jnp.int32) + has(1).astype(jnp.int32)
    near_count = near_count + 3 * (last_z & has(1)).astype(jnp.int32)
    pl.semaphore_wait(barrier, group * MEMBERS + (MEMBERS - 1) + near_count)

    def send_place(to_group, to_member):
        pltpu.make_async_remote_copy(
            src_ref=send_p.at[to_group * MEMBERS + to_member],
            dst_ref=recv_p.at[group, member],
            send_sem=send_sem.at[0],
            recv_sem=recv_p_sem.at[group],
            device_id={"leaf": peer(to_group, to_member)},
            device_id_type=MESH,
        ).start()

    def send_value(to_group, to_member):
        pltpu.make_async_remote_copy(
            src_ref=send_v.at[to_group * MEMBERS + to_member],
            dst_ref=recv_v.at[group, member],
            send_sem=send_sem.at[1],
            recv_sem=recv_v_sem.at[group],
            device_id={"leaf": peer(to_group, to_member)},
            device_id_type=MESH,
        ).start()

    def places_to(to_group, carry):
        for m in range(MEMBERS):
            send_place(to_group, m)
        return carry

    def values_to(to_group, carry):
        for m in range(MEMBERS):
            send_value(to_group, m)
        return carry

    own_quad = group // QUAD

    own_rows = pl.ds(pl.multiple_of(sub * 16, 16), 16)

    def pass_on(source, place, target, sems):
        pltpu.make_async_remote_copy(
            src_ref=source,
            dst_ref=window.at[pl.ds(place * 4, 4), own_rows, :],
            send_sem=near_sem.at[sems],
            recv_sem=near_sem.at[sems + 1],
            device_id=target,
            device_id_type=MESH,
        ).start()

    def window_part(place, count):
        return window.at[pl.ds(place * 4, 4), pl.ds(0, 16 * count), :]

    def wait_window(place, count, sem):
        part = window_part(place, count)
        pltpu.make_async_copy(part, part, near_sem.at[sem]).wait()

    for shift in (-1, 1):

        @pl.when(has(shift))
        def _():
            pass_on(v_own, 1 - shift, {"leaf": me + shift}, 2 * (1 - shift))

    @pl.when(last_z & has(1))
    def _():
        for target in across_after:
            pass_on(v_own, 0, target, 0)

    ahead = jnp.minimum(own_quad, 1) * QUAD
    lax.fori_loop(0, group, places_to, 0)
    for n in range(1, MEMBERS):
        send_place(group, (member + n) % MEMBERS)
    lax.fori_loop(0, ahead, values_to, 0)

    for target in across_sub:
        pass_on(v_own, 1, target, 2)

    lax.fori_loop(ahead, group, values_to, 0)
    for n in range(1, MEMBERS):
        send_value(group, (member + n) % MEMBERS)

    for place in (0, 2):

        @pl.when(jnp.logical_not(has(place - 1)))
        def _():
            window[place * 4 : place * 4 + 4] = jnp.zeros((4, 64, 256), BF16)

    window[4:8, own_rows, :] = v_own[...]
    mine = group * MEMBERS + member
    recv_v[group, member] = send_v[mine]
    recv_p[group, member] = send_p[mine]

    down[...] = jnp.zeros((256, 1024), BF16)
    first_dims = (((0,), (0,)), ((), ()))
    for leaf in range(4):
        at = slice(leaf * 256, (leaf + 1) * 256)
        down[leaf * 32 : leaf * 32 + 32, at] = v_basis[leaf]
        once = lax.dot_general(v_map[leaf], v_basis[leaf], first_dims, preferred_element_type=F32).astype(BF16)
        parent = 4 + leaf // 2
        down[parent * 32 : parent * 32 + 32, at] = once
        twice = lax.dot_general(v_map[parent], once, first_dims, preferred_element_type=F32)
        down[192:224, at] = twice.astype(BF16)
    acc[...] = jnp.zeros((64, 128), F32)
    loads[5].wait()
    loads[6].wait()
    loads[7].wait()

    def take(quad):
        first = pl.multiple_of(quad * QUAD, QUAD)
        got = recv_p[pl.ds(first, QUAD)].reshape(32, 32)
        values = recv_v[pl.ds(first, QUAD)].astype(F32).reshape(256, 128).astype(BF16)
        row_in = (iota((32, 128), 1) % 8).astype(F32)
        sums = []
        for slot in range(2):
            each = got[:, slot * 16 : slot * 16 + 1] * 8.0 + row_in
            row = []
            for tile in range(2):
                own = iota((16, 128), 0) == iota((16, 128), 1) // 8
                part = each[tile * 16 : tile * 16 + 16]
                row.append(jnp.sum(jnp.where(own, part, 0.0), axis=0, keepdims=True))
            row = jnp.concatenate(row, axis=1)
            weight = jnp.where(fiota((64, 256), 0) == row, 1.0, 0.0).astype(BF16)
            sums.append(jnp.dot(weight, values, preferred_element_type=F32))
        acc[...] += jnp.where(iota((64, 128), 1) < 64, sums[0], sums[1])

    def wait_from(ref, sems, from_group, count):
        part = ref.at[from_group, pl.ds(0, count)]
        pltpu.make_async_copy(part, part, sems.at[from_group]).wait()

    def answer(from_group, carry):
        wait_from(recv_p, recv_p_sem, from_group, MEMBERS)
        for m in range(MEMBERS):
            send_place(from_group, m)
            send_value(from_group, m)
        return carry

    def forward(place):
        wait_window(place, 1, 2 * place + 1)
        for target in across_sub:
            pass_on(window.at[pl.ds(place * 4, 4), own_rows, :], place, target, 6 + place)

    pl.when(has(1))(lambda: forward(2))
    pl.when(has(-1) & jnp.logical_not(first_z))(lambda: forward(0))

    lax.fori_loop(group + 1, own_quad * QUAD + QUAD, answer, 0)

    last = jnp.maximum(own_quad * QUAD + QUAD, GROUPS - QUAD)
    lax.fori_loop(own_quad * QUAD + QUAD, last, answer, 0)

    wait_window(1, 3, 3)
    pl.when(has(1))(lambda: wait_window(2, 3, 9))
    pl.when(has(-1) & jnp.logical_not(first_z))(lambda: wait_window(0, 3, 7))
    pl.when(has(-1) & first_z)(lambda: wait_window(0, 4, 1))

    near = jnp.zeros((64, 256), F32)
    for k in range(9):
        source = window[jnp.clip(s_cols[0, k] - (me - 1) * 4, 0, 11)]
        keep = s_mask[0, k].astype(F32)
        near = near + keep * jnp.dot(source, v_blk[k], preferred_element_type=F32)
    near_out[...] = near.reshape(4, 16, 256)
    for turn in range(1, SUBS):
        pltpu.make_async_remote_copy(
            src_ref=near_out.at[(sub + turn) % SUBS],
            dst_ref=near_in.at[sub],
            send_sem=near_sem.at[10],
            recv_sem=near_sem.at[11],
            device_id={"sub": (sub + turn) % SUBS},
            device_id_type=MESH,
        ).start()
    near_in[sub] = near_out[sub]

    def hear(from_group, carry):
        own = from_group == group

        @pl.when(own)
        def _():
            wait_from(recv_p, recv_p_sem, from_group, MEMBERS - 1)
            wait_from(recv_v, recv_v_sem, from_group, MEMBERS - 1)

        @pl.when(from_group < group)
        def _():
            wait_from(recv_p, recv_p_sem, from_group, MEMBERS)

        @pl.when(jnp.logical_not(own))
        def _():
            wait_from(recv_v, recv_v_sem, from_group, MEMBERS)

        return carry

    def hear_quad(quad, carry):
        lax.fori_loop(quad * QUAD, quad * QUAD + QUAD, hear, 0)
        take(quad)
        return carry

    lax.fori_loop(own_quad, jnp.maximum(own_quad + 1, QUADS - 1), hear_quad, 0)

    lax.fori_loop(last, GROUPS, answer, 0)

    lax.fori_loop(jnp.maximum(own_quad + 1, QUADS - 1), QUADS, hear_quad, 0)
    lax.fori_loop(0, own_quad, hear_quad, 0)

    total = acc[...]
    total = total + pltpu.roll(total, 64, 1)
    lane_group = iota((8, 128), 1) // 32
    halves = []
    for high in range(2):
        tiles = []
        for tile in range(2):
            mixed = jnp.zeros((8, 128), F32)
            for lg in range(4):
                c = tile * 4 + lg
                if c < 7:
                    part = total[c * 8 : c * 8 + 8, :]
                    turn = (lg * 32 - high * 32) % 128
                    part = pltpu.roll(part, turn, 1) if turn else part
                    mixed = jnp.where(lane_group == lg, part, mixed)
            tiles.append(mixed)
        halves.append(jnp.concatenate(tiles, axis=1))
    far = wide_dot(jnp.concatenate(halves, axis=0), down[...])
    pltpu.make_async_copy(near_in.at[pl.ds(0, 3)], near_in.at[pl.ds(0, 3)], near_sem.at[11]).wait()
    for leaf in range(4):
        at = slice(leaf * 256, (leaf + 1) * 256)
        out[:, at] = (near_in[leaf] + far[:, at]).astype(BF16)

    pltpu.make_async_copy(send_p.at[pl.ds(0, 127)], send_p.at[pl.ds(0, 127)], send_sem.at[0]).wait()
    pltpu.make_async_copy(send_v.at[pl.ds(0, 127)], send_v.at[pl.ds(0, 127)], send_sem.at[1]).wait()
    wait_window(1, 3, 2)
    pl.when(has(-1))(lambda: wait_window(2, 1, 4))
    pl.when(has(1) & jnp.logical_not(last_z))(lambda: wait_window(0, 1, 0))
    pl.when(has(1) & last_z)(lambda: wait_window(0, 4, 0))
    pl.when(has(1))(lambda: wait_window(2, 3, 8))
    pl.when(has(-1) & jnp.logical_not(first_z))(lambda: wait_window(0, 3, 6))
    pltpu.make_async_copy(near_out.at[pl.ds(0, 3)], near_out.at[pl.ds(0, 3)], near_sem.at[10]).wait()


def local(*args):
    any_space = pl.BlockSpec(memory_space=pl.ANY)
    dma = pltpu.SemaphoreType.DMA
    vmem = pltpu.VMEM
    return pl.pallas_call(
        kernel,
        out_shape=jax.ShapeDtypeStruct((16, 1024), BF16),
        in_specs=[any_space] * 9,
        out_specs=pl.BlockSpec(memory_space=pltpu.VMEM),
        scratch_shapes=[
            vmem((4, 16, 256), BF16),
            vmem((9, 256, 256), BF16),
            vmem((4, 32, 256), BF16),
            vmem((6, 32, 32), BF16),
            vmem((7, 32, 32, 32), BF16),
            vmem((7, 27), jnp.int32),
            vmem((7, 27), jnp.int32),
            vmem((2, 8, 128), F32),
            vmem((896, 128), F32),
            vmem((256, 512), BF16),
            vmem((1024, 128), F32),
            vmem((128, 8, 128), BF16),
            vmem((128, 1, 32), F32),
            vmem((16, 8, 8, 128), BF16),
            vmem((16, 8, 1, 32), F32),
            vmem((12, 64, 256), BF16),
            vmem((4, 16, 256), F32),
            vmem((4, 16, 256), F32),
            vmem((256, 1024), BF16),
            vmem((64, 128), F32),
            pltpu.SMEM((1, 9), jnp.int32),
            pltpu.SMEM((1, 9), jnp.int32),
            dma((12,)),
            dma((2,)),
            dma((16,)),
            dma((16,)),
            dma((12,)),
        ],
        compiler_params=pltpu.CompilerParams(collective_id=0, has_side_effects=True),
    )(*args)


def solution(mesh):
    return jax.shard_map(
        local,
        mesh=mesh,
        in_specs=(
            P("sub", "leaf"),
            P(("leaf", "sub"), None, None, None),
            P(("leaf", "sub"), None),
            P(("leaf", "sub"), None),
            P("leaf", None, None),
            P("leaf", None, None),
            P("leaf", None, None, None),
            P("leaf", None),
            P("leaf", None),
        ),
        out_specs=P("sub", "leaf"),
        check_vma=False,
    )
```

time: 38.1 us -> 32.6 us (0.86)
  the two profiles are of different devices: /device:TPU:8 before, /device:TPU:36 now
where the time goes in v2:
time: 32.6 us; the launch traced here: 32.4 us
  Pallas kernels  31 us (95%)
  local copies, waits for them, and re-layouts  1.38 us (4%)
    pallas_call x1, Pallas kernels, local(): pl.pallas_call(kernel, out_shape=jax.ShapeDtypeStruct((16, 1024), BF16),...  31 us
    unnamed x1, local copies, waits for them, and re-layouts  1.38 us

profile of v2, /device:TPU:36, one launch (start us, length us, event | category | flops | bytes accessed | tf_op | source)
XLA Modules:
  0.0 32.4 jit_solution(4012450032222701753)
XLA Ops:
  0.0 31.0 %shard_map.91 = bf16[16,1024]{1,0:T(8,128)(2,1)} custom-call(bf16[16,1024]{1,0:T(8,128)(2,1)} %vec.1, bf16[1,9,256,256]{3,2,1,0:T(8,128)(2,1)} %blocks.1, s32[1,9]{1,0:T(1,128)} %near_cols.1, s32[1,9]{1,0:T(1,128)} %near_mask.1, bf16[4,32,256]{2,1,0:T(8,128)(2,1)} %basis.1, bf16[6,32,32]{2,1,0:T(8,128)(2,1)} %transfer.1, bf16[7,27,32,32]{3,2,1,0:T(8,128)(2,1)} %coupling.1, ...), custom_call_target="tpu_custom_call" | custom-call | tf_op jit(solution)/shard_map/pallas_call | solution.py:481
  31.0 1.4 %copy.11 = bf16[16,1024]{1,0:T(8,128)(2,1)} copy(bf16[16,1024]{1,0:T(8,128)(2,1)} %shard_map.91) | data formatting | bytes 65536

commit v3 on v2

--- a/solution.py
+++ b/solution.py
@@ -133,8 +133,8 @@
         pltpu.make_async_copy(vec.at[:, pl.ds(leaf * 256, 256)], v_own.at[leaf], load_sem.at[8 + leaf])
         for leaf in range(4)
     ]
-    for copy in loads:
-        copy.start()
+    for n in (0, 1, 8, 9, 10, 11, 2, 3, 4, 5, 6, 7):
+        loads[n].start()
 
     barrier = pltpu.get_barrier_semaphore()
 
@@ -151,10 +151,9 @@
 
     across_sub = [{"sub": (sub + turn) % SUBS} for turn in range(1, SUBS)]
 
-    first_z = me % 16 == 0
-    last_z = me % 16 == 15
-    across_after = [{"leaf": me + 1, "sub": (sub + turn) % SUBS} for turn in range(1, SUBS)]
-    across_before = [{"leaf": me - 1, "sub": (sub + turn) % SUBS} for turn in range(1, SUBS)]
+    late_before = (me % 16 == 0) & has(-1)
+    late_after = me % 16 == 7
+    late_side = late_before | late_after
 
     def near_peers(shift):
         return across_sub if shift == 0 else [{"leaf": me + shift}]
@@ -165,11 +164,6 @@
         def _():
             for target in near_peers(shift):
                 pl.semaphore_signal(barrier, inc=1, device_id=target, device_id_type=MESH)
-
-    @pl.when(first_z & has(-1))
-    def _():
-        for target in across_before:
-            pl.semaphore_signal(barrier, inc=1, device_id=target, device_id_type=MESH)
 
     def greet_later(n, carry):
         for m in range(MEMBERS):
@@ -242,7 +236,6 @@
     send_v[...] = slabs[...].reshape(128, 8, 128).astype(BF16)
 
     near_count = 3 + has(-1).astype(jnp.int32) + has(1).astype(jnp.int32)
-    near_count = near_count + 3 * (last_z & has(1)).astype(jnp.int32)
     pl.semaphore_wait(barrier, group * MEMBERS + (MEMBERS - 1) + near_count)
 
     def send_place(to_group, to_member):
@@ -265,14 +258,19 @@
             device_id_type=MESH,
         ).start()
 
-    def places_to(to_group, carry):
+    def turned(n):
+        return jnp.where(n // QUAD < group // QUAD, (n // QUAD) * QUAD + (n + group) % QUAD, n)
+
+    def places_to(n, carry):
+        to_group = turned(n)
         for m in range(MEMBERS):
-            send_place(to_group, m)
+            send_place(to_group, (member + m) % MEMBERS)
         return carry
 
-    def values_to(to_group, carry):
+    def values_to(n, carry):
+        to_group = turned(n)
         for m in range(MEMBERS):
-            send_value(to_group, m)
+            send_value(to_group, (member + m) % MEMBERS)
         return carry
 
     own_quad = group // QUAD
@@ -302,16 +300,12 @@
         def _():
             pass_on(v_own, 1 - shift, {"leaf": me + shift}, 2 * (1 - shift))
 
-    @pl.when(last_z & has(1))
-    def _():
-        for target in across_after:
-            pass_on(v_own, 0, target, 0)
-
     ahead = jnp.minimum(own_quad, 1) * QUAD
-    lax.fori_loop(0, group, places_to, 0)
+    lax.fori_loop(0, ahead, places_to, 0)
+    lax.fori_loop(0, ahead, values_to, 0)
+    lax.fori_loop(ahead, group, places_to, 0)
     for n in range(1, MEMBERS):
         send_place(group, (member + n) % MEMBERS)
-    lax.fori_loop(0, ahead, values_to, 0)
 
     for target in across_sub:
         pass_on(v_own, 1, target, 2)
@@ -371,8 +365,8 @@
     def answer(from_group, carry):
         wait_from(recv_p, recv_p_sem, from_group, MEMBERS)
         for m in range(MEMBERS):
-            send_place(from_group, m)
-            send_value(from_group, m)
+            send_place(from_group, (member + m) % MEMBERS)
+            send_value(from_group, (member + m) % MEMBERS)
         return carry
 
     def forward(place):
@@ -380,35 +374,29 @@
         for target in across_sub:
             pass_on(window.at[pl.ds(place * 4, 4), own_rows, :], place, target, 6 + place)
 
-    pl.when(has(1))(lambda: forward(2))
-    pl.when(has(-1) & jnp.logical_not(first_z))(lambda: forward(0))
-
-    lax.fori_loop(group + 1, own_quad * QUAD + QUAD, answer, 0)
-
-    last = jnp.maximum(own_quad * QUAD + QUAD, GROUPS - QUAD)
-    lax.fori_loop(own_quad * QUAD + QUAD, last, answer, 0)
-
-    wait_window(1, 3, 3)
-    pl.when(has(1))(lambda: wait_window(2, 3, 9))
-    pl.when(has(-1) & jnp.logical_not(first_z))(lambda: wait_window(0, 3, 7))
-    pl.when(has(-1) & first_z)(lambda: wait_window(0, 4, 1))
-
-    near = jnp.zeros((64, 256), F32)
-    for k in range(9):
-        source = window[jnp.clip(s_cols[0, k] - (me - 1) * 4, 0, 11)]
-        keep = s_mask[0, k].astype(F32)
-        near = near + keep * jnp.dot(source, v_blk[k], preferred_element_type=F32)
-    near_out[...] = near.reshape(4, 16, 256)
-    for turn in range(1, SUBS):
-        pltpu.make_async_remote_copy(
-            src_ref=near_out.at[(sub + turn) % SUBS],
-            dst_ref=near_in.at[sub],
-            send_sem=near_sem.at[10],
-            recv_sem=near_sem.at[11],
-            device_id={"sub": (sub + turn) % SUBS},
-            device_id_type=MESH,
-        ).start()
-    near_in[sub] = near_out[sub]
+    pl.when(has(1) & jnp.logical_not(late_after))(lambda: forward(2))
+    pl.when(has(-1) & jnp.logical_not(late_before))(lambda: forward(0))
+
+    def near_field():
+        wait_window(1, 3, 3)
+        pl.when(has(1))(lambda: wait_window(2, 3, 9))
+        pl.when(has(-1))(lambda: wait_window(0, 3, 7))
+        near = jnp.zeros((64, 256), F32)
+        for k in range(9):
+            source = window[jnp.clip(s_cols[0, k] - (me - 1) * 4, 0, 11)]
+            keep = s_mask[0, k].astype(F32)
+            near = near + keep * jnp.dot(source, v_blk[k], preferred_element_type=F32)
+        near_out[...] = near.reshape(4, 16, 256)
+        for turn in range(1, SUBS):
+            pltpu.make_async_remote_copy(
+                src_ref=near_out.at[(sub + turn) % SUBS],
+                dst_ref=near_in.at[sub],
+                send_sem=near_sem.at[10],
+                recv_sem=near_sem.at[11],
+                device_id={"sub": (sub + turn) % SUBS},
+                device_id_type=MESH,
+            ).start()
+        near_in[sub] = near_out[sub]
 
     def hear(from_group, carry):
         own = from_group == group
@@ -433,12 +421,23 @@
         take(quad)
         return carry
 
-    lax.fori_loop(own_quad, jnp.maximum(own_quad + 1, QUADS - 1), hear_quad, 0)
-
-    lax.fori_loop(last, GROUPS, answer, 0)
-
-    lax.fori_loop(jnp.maximum(own_quad + 1, QUADS - 1), QUADS, hear_quad, 0)
-    lax.fori_loop(0, own_quad, hear_quad, 0)
+    early = own_quad < 2
+    split = jnp.where(early, 2 * QUAD, GROUPS)
+    lax.fori_loop(group + 1, split, answer, 0)
+
+    pl.when(jnp.logical_not(late_side))(near_field)
+
+    lax.fori_loop(own_quad, 2, hear_quad, 0)
+
+    pl.when(late_before)(lambda: forward(0))
+    pl.when(late_after)(lambda: forward(2))
+
+    lax.fori_loop(split, GROUPS, answer, 0)
+
+    pl.when(late_side)(near_field)
+
+    lax.fori_loop(2, QUADS, hear_quad, 0)
+    lax.fori_loop(0, jnp.minimum(own_quad, 2), hear_quad, 0)
 
     total = acc[...]
     total = total + pltpu.roll(total, 64, 1)
@@ -467,15 +466,15 @@
     pltpu.make_async_copy(send_v.at[pl.ds(0, 127)], send_v.at[pl.ds(0, 127)], send_sem.at[1]).wait()
     wait_window(1, 3, 2)
     pl.when(has(-1))(lambda: wait_window(2, 1, 4))
-    pl.when(has(1) & jnp.logical_not(last_z))(lambda: wait_window(0, 1, 0))
-    pl.when(has(1) & last_z)(lambda: wait_window(0, 4, 0))
+    pl.when(has(1))(lambda: wait_window(0, 1, 0))
     pl.when(has(1))(lambda: wait_window(2, 3, 8))
-    pl.when(has(-1) & jnp.logical_not(first_z))(lambda: wait_window(0, 3, 6))
+    pl.when(has(-1))(lambda: wait_window(0, 3, 6))
     pltpu.make_async_copy(near_out.at[pl.ds(0, 3)], near_out.at[pl.ds(0, 3)], near_sem.at[10]).wait()
 
 
 def local(*args):
-    any_space = pl.BlockSpec(memory_space=pl.ANY)
+    args = [pltpu.with_memory_space_constraint(array, pltpu.HBM) for array in args]
+    any_space = pl.BlockSpec(memory_space=pltpu.HBM)
     dma = pltpu.SemaphoreType.DMA
     vmem = pltpu.VMEM
     return pl.pallas_call(
@@ -512,7 +511,9 @@
             dma((16,)),
             dma((12,)),
         ],
-        compiler_params=pltpu.CompilerParams(collective_id=0, has_side_effects=True),
+        compiler_params=pltpu.CompilerParams(
+            collective_id=0, has_side_effects=True, vmem_limit_bytes=16 * 1024 * 1024
+        ),
     )(*args)
 
 

time: 32.6 us -> 30.3 us (0.929)
  the two profiles are of different devices: /device:TPU:36 before, /device:TPU:56 now
where the time goes in v3:
time: 30.3 us; the launch traced here: 30.2 us
  Pallas kernels  29.6 us (98%)
  local copies, waits for them, and re-layouts  0.62 us (2%)
    pallas_call x1, Pallas kernels, local(): pl.pallas_call(kernel, out_shape=jax.ShapeDtypeStruct((16, 1024), BF16),...  29.6 us
    unnamed x1, local copies, waits for them, and re-layouts  0.62 us

profile of v3, /device:TPU:56, one launch (start us, length us, event | category | flops | bytes accessed | tf_op | source)
XLA Modules:
  0.0 30.2 jit_solution(2930120741304446269)
XLA Ops:
  0.0 29.6 %shard_map.91 = bf16[16,1024]{1,0:T(8,128)(2,1)S(1)} custom-call(bf16[16,1024]{1,0:T(8,128)(2,1)} %vec.1, bf16[1,9,256,256]{3,2,1,0:T(8,128)(2,1)} %blocks.1, s32[1,9]{1,0:T(1,128)} %near_cols.1, s32[1,9]{1,0:T(1,128)} %near_mask.1, bf16[4,32,256]{2,1,0:T(8,128)(2,1)} %basis.1, bf16[6,32,32]{2,1,0:T(8,128)(2,1)} %transfer.1, ...), custom_call_target="tpu_custom_call" | custom-call | tf_op jit(solution)/shard_map/pallas_call | solution.py:480
  29.6 0.6 %copy.11 = bf16[16,1024]{1,0:T(8,128)(2,1)} copy(bf16[16,1024]{1,0:T(8,128)(2,1)S(1)} %shard_map.91) | data formatting | bytes 65536

commit v4 on v3

--- a/solution.py
+++ b/solution.py
@@ -12,6 +12,7 @@
 MEMBERS = 8
 QUAD = 4
 QUADS = GROUPS // QUAD
+LOWER = GROUPS // 2
 LEAVES = 128
 SUBS = 4
 
@@ -102,23 +103,34 @@
     send_p,
     recv_v,
     recv_p,
+    for_v,
+    for_p,
+    joint,
+    joined,
     window,
     near_out,
     near_in,
     down,
     acc,
+    acc_for,
     s_cols,
     s_mask,
     load_sem,
     send_sem,
     recv_v_sem,
     recv_p_sem,
+    for_v_sem,
+    for_p_sem,
+    joined_sem,
     near_sem,
 ):
     me = lax.axis_index("leaf")
     sub = lax.axis_index("sub")
     group = ((me // 8) % 2) * 8 + (me // 64) * 4 + (me // 2) % 4
     member = ((me // 16) % 4) * 2 + me % 2
+    own_quad = group // QUAD
+    in_quad = group % QUAD
+    early = group < LOWER
 
     loads = [
         pltpu.make_async_copy(far_targets, v_tgt, load_sem.at[0]),
@@ -170,6 +182,7 @@
             greet(n, m)
         return carry
 
+    lax.fori_loop(jnp.where(early, own_quad * QUAD, group), group, greet_later, 0)
     lax.fori_loop(group + 1, GROUPS, greet_later, 0)
 
     v_coup[:, 27:32] = jnp.zeros((7, 5, 32, 32), BF16)
@@ -236,7 +249,8 @@
     send_v[...] = slabs[...].reshape(128, 8, 128).astype(BF16)
 
     near_count = 3 + has(-1).astype(jnp.int32) + has(1).astype(jnp.int32)
-    pl.semaphore_wait(barrier, group * MEMBERS + (MEMBERS - 1) + near_count)
+    heard = jnp.where(early, (own_quad + 1) * QUAD, group + 1) * MEMBERS - 1
+    pl.semaphore_wait(barrier, heard + near_count)
 
     def send_place(to_group, to_member):
         pltpu.make_async_remote_copy(
@@ -258,6 +272,26 @@
             device_id_type=MESH,
         ).start()
 
+    def partner_group(half):
+        return LOWER + half * QUAD + group % QUAD
+
+    def send_for(to_group, to_member):
+        for half in range(2):
+            partner = (LOWER + half * QUAD + to_group % QUAD) * MEMBERS + to_member
+            place = half * QUAD + group % QUAD
+            for source, target, sems, which in (
+                (send_p, for_p, for_p_sem, 2),
+                (send_v, for_v, for_v_sem, 3),
+            ):
+                pltpu.make_async_remote_copy(
+                    src_ref=source.at[partner],
+                    dst_ref=target.at[place, member],
+                    send_sem=send_sem.at[which],
+                    recv_sem=sems.at[place],
+                    device_id={"leaf": peer(to_group, to_member)},
+                    device_id_type=MESH,
+                ).start()
+
     def turned(n):
         return jnp.where(n // QUAD < group // QUAD, (n // QUAD) * QUAD + (n + group) % QUAD, n)
 
@@ -272,8 +306,6 @@
         for m in range(MEMBERS):
             send_value(to_group, (member + m) % MEMBERS)
         return carry
-
-    own_quad = group // QUAD
 
     own_rows = pl.ds(pl.multiple_of(sub * 16, 16), 16)
 
@@ -300,17 +332,39 @@
         def _():
             pass_on(v_own, 1 - shift, {"leaf": me + shift}, 2 * (1 - shift))
 
+    mine = group * MEMBERS + member
+    def beside(n, carry):
+        to_group = own_quad * QUAD + (in_quad + n) % QUAD
+        for m in range(MEMBERS):
+            send_for(to_group, (member + m) % MEMBERS)
+        for m in range(MEMBERS):
+            send_place(to_group, (member + m) % MEMBERS)
+            send_value(to_group, (member + m) % MEMBERS)
+        return carry
+
     ahead = jnp.minimum(own_quad, 1) * QUAD
     lax.fori_loop(0, ahead, places_to, 0)
+
+    @pl.when(early)
+    def _():
+        lax.fori_loop(1, QUAD, beside, 0)
+        for n in range(1, MEMBERS):
+            send_for(group, (member + n) % MEMBERS)
+        for half in range(2):
+            partner = partner_group(half) * MEMBERS + member
+            for_v[half * QUAD + in_quad, member] = send_v[partner]
+            for_p[half * QUAD + in_quad, member] = send_p[partner]
+
     lax.fori_loop(0, ahead, values_to, 0)
-    lax.fori_loop(ahead, group, places_to, 0)
+    rest = jnp.where(early, ahead, group)
+    lax.fori_loop(ahead, rest, places_to, 0)
     for n in range(1, MEMBERS):
         send_place(group, (member + n) % MEMBERS)
 
     for target in across_sub:
         pass_on(v_own, 1, target, 2)
 
-    lax.fori_loop(ahead, group, values_to, 0)
+    lax.fori_loop(ahead, rest, values_to, 0)
     for n in range(1, MEMBERS):
         send_value(group, (member + n) % MEMBERS)
 
@@ -321,7 +375,6 @@
             window[place * 4 : place * 4 + 4] = jnp.zeros((4, 64, 256), BF16)
 
     window[4:8, own_rows, :] = v_own[...]
-    mine = group * MEMBERS + member
     recv_v[group, member] = send_v[mine]
     recv_p[group, member] = send_p[mine]
 
@@ -336,14 +389,15 @@
         twice = lax.dot_general(v_map[parent], once, first_dims, preferred_element_type=F32)
         down[192:224, at] = twice.astype(BF16)
     acc[...] = jnp.zeros((64, 128), F32)
+    acc_for[...] = jnp.zeros((2, 64, 128), F32)
     loads[5].wait()
     loads[6].wait()
     loads[7].wait()
 
-    def take(quad):
+    def take(quad, from_p, from_v, total):
         first = pl.multiple_of(quad * QUAD, QUAD)
-        got = recv_p[pl.ds(first, QUAD)].reshape(32, 32)
-        values = recv_v[pl.ds(first, QUAD)].astype(F32).reshape(256, 128).astype(BF16)
+        got = from_p[pl.ds(first, QUAD)].reshape(32, 32)
+        values = from_v[pl.ds(first, QUAD)].astype(F32).reshape(256, 128).astype(BF16)
         row_in = (iota((32, 128), 1) % 8).astype(F32)
         sums = []
         for slot in range(2):
@@ -356,7 +410,7 @@
             row = jnp.concatenate(row, axis=1)
             weight = jnp.where(fiota((64, 256), 0) == row, 1.0, 0.0).astype(BF16)
             sums.append(jnp.dot(weight, values, preferred_element_type=F32))
-        acc[...] += jnp.where(iota((64, 128), 1) < 64, sums[0], sums[1])
+        total[...] += jnp.where(iota((64, 128), 1) < 64, sums[0], sums[1])
 
     def wait_from(ref, sems, from_group, count):
         part = ref.at[from_group, pl.ds(0, count)]
@@ -367,6 +421,7 @@
         for m in range(MEMBERS):
             send_place(from_group, (member + m) % MEMBERS)
             send_value(from_group, (member + m) % MEMBERS)
+
         return carry
 
     def forward(place):
@@ -398,46 +453,94 @@
             ).start()
         near_in[sub] = near_out[sub]
 
-    def hear(from_group, carry):
+    first = jnp.where(early, own_quad * QUAD + QUAD, group + 1)
+    lax.fori_loop(first, jnp.where(early, LOWER, GROUPS), answer, 0)
+
+    pl.when(jnp.logical_not(late_side))(near_field)
+
+    def hear_from(refs, from_group):
         own = from_group == group
 
         @pl.when(own)
         def _():
-            wait_from(recv_p, recv_p_sem, from_group, MEMBERS - 1)
-            wait_from(recv_v, recv_v_sem, from_group, MEMBERS - 1)
-
-        @pl.when(from_group < group)
-        def _():
-            wait_from(recv_p, recv_p_sem, from_group, MEMBERS)
+            for ref, sems in refs:
+                wait_from(ref, sems, from_group, MEMBERS - 1)
 
         @pl.when(jnp.logical_not(own))
         def _():
-            wait_from(recv_v, recv_v_sem, from_group, MEMBERS)
+            for ref, sems in refs:
+                wait_from(ref, sems, from_group, MEMBERS)
+
+    def hear(from_group, carry):
+        answered = (from_group >= first) & ((from_group < LOWER) | jnp.logical_not(early))
+        answered = answered | (early & (from_group >= LOWER) & (from_group % QUAD == group % QUAD))
+        pl.when(answered)(lambda: wait_from(recv_v, recv_v_sem, from_group, MEMBERS))
+        pl.when(jnp.logical_not(answered))(
+            lambda: hear_from(((recv_p, recv_p_sem), (recv_v, recv_v_sem)), from_group)
+        )
+        return carry
+
+    def hear_for(place, carry):
+        refs = ((for_p, for_p_sem), (for_v, for_v_sem))
+        own = place % QUAD == group % QUAD
+
+        @pl.when(own)
+        def _():
+            for ref, sems in refs:
+                wait_from(ref, sems, place, MEMBERS - 1)
+
+        @pl.when(jnp.logical_not(own))
+        def _():
+            for ref, sems in refs:
+                wait_from(ref, sems, place, MEMBERS)
 
         return carry
 
     def hear_quad(quad, carry):
         lax.fori_loop(quad * QUAD, quad * QUAD + QUAD, hear, 0)
-        take(quad)
-        return carry
-
-    early = own_quad < 2
-    split = jnp.where(early, 2 * QUAD, GROUPS)
-    lax.fori_loop(group + 1, split, answer, 0)
-
-    pl.when(jnp.logical_not(late_side))(near_field)
-
-    lax.fori_loop(own_quad, 2, hear_quad, 0)
+        take(quad, recv_p, recv_v, acc)
+        return carry
+
+    low = iota((32, 128), 1) < 64
 
     pl.when(late_before)(lambda: forward(0))
     pl.when(late_after)(lambda: forward(2))
 
-    lax.fori_loop(split, GROUPS, answer, 0)
+    @pl.when(early)
+    def _():
+        lax.fori_loop(0, 2 * QUAD, hear_for, 0)
+        for half in range(2):
+            take(half, for_p, for_v, acc_for.at[half])
+            both = acc_for[half] + pltpu.roll(acc_for[half], 64, 1)
+            joint[half] = jnp.where(low, both[0:32], both[32:64])
+
+    lax.fori_loop(own_quad, 2, hear_quad, 0)
 
     pl.when(late_side)(near_field)
 
+    @pl.when(early)
+    def _():
+        for half in range(2):
+            wait_from(recv_p, recv_p_sem, partner_group(half), MEMBERS)
+            pltpu.make_async_remote_copy(
+                src_ref=joint.at[half],
+                dst_ref=joined.at[own_quad % 2],
+                send_sem=send_sem.at[4],
+                recv_sem=joined_sem.at[own_quad % 2],
+                device_id={"leaf": peer(partner_group(half), member)},
+                device_id_type=MESH,
+            ).start()
+
     lax.fori_loop(2, QUADS, hear_quad, 0)
-    lax.fori_loop(0, jnp.minimum(own_quad, 2), hear_quad, 0)
+    lax.fori_loop(0, own_quad % 2 * early.astype(jnp.int32), hear_quad, 0)
+
+    @pl.when(jnp.logical_not(early))
+    def _():
+        for quad in range(2):
+            pltpu.make_async_copy(joined.at[quad], joined.at[quad], joined_sem.at[quad]).wait()
+        both = joined[0] + joined[1]
+        acc[0:32] += jnp.where(low, both, 0.0)
+        acc[32:64] += jnp.where(low, 0.0, both)
 
     total = acc[...]
     total = total + pltpu.roll(total, 64, 1)
@@ -462,8 +565,23 @@
         at = slice(leaf * 256, (leaf + 1) * 256)
         out[:, at] = (near_in[leaf] + far[:, at]).astype(BF16)
 
-    pltpu.make_async_copy(send_p.at[pl.ds(0, 127)], send_p.at[pl.ds(0, 127)], send_sem.at[0]).wait()
-    pltpu.make_async_copy(send_v.at[pl.ds(0, 127)], send_v.at[pl.ds(0, 127)], send_sem.at[1]).wait()
+    def sent(ref, count, sem):
+        part = ref.at[pl.ds(0, count)]
+        pltpu.make_async_copy(part, part, send_sem.at[sem]).wait()
+
+    @pl.when(early)
+    def _():
+        for ref, sem in ((send_p, 0), (send_v, 1)):
+            sent(ref, LOWER * MEMBERS - 1, sem)
+        for ref, sem in ((send_p, 2), (send_v, 3)):
+            sent(ref, 2 * (QUAD * MEMBERS - 1), sem)
+        sent(joint, 2, 4)
+
+    @pl.when(jnp.logical_not(early))
+    def _():
+        for ref, sem in ((send_p, 0), (send_v, 1)):
+            sent(ref, GROUPS * MEMBERS - 1, sem)
+
     wait_window(1, 3, 2)
     pl.when(has(-1))(lambda: wait_window(2, 1, 4))
     pl.when(has(1))(lambda: wait_window(0, 1, 0))
@@ -498,17 +616,25 @@
             vmem((128, 1, 32), F32),
             vmem((16, 8, 8, 128), BF16),
             vmem((16, 8, 1, 32), F32),
+            vmem((8, 8, 8, 128), BF16),
+            vmem((8, 8, 1, 32), F32),
+            vmem((2, 32, 128), F32),
+            vmem((2, 32, 128), F32),
             vmem((12, 64, 256), BF16),
             vmem((4, 16, 256), F32),
             vmem((4, 16, 256), F32),
             vmem((256, 1024), BF16),
             vmem((64, 128), F32),
+            vmem((2, 64, 128), F32),
             pltpu.SMEM((1, 9), jnp.int32),
             pltpu.SMEM((1, 9), jnp.int32),
             dma((12,)),
-            dma((2,)),
+            dma((5,)),
             dma((16,)),
             dma((16,)),
+            dma((8,)),
+            dma((8,)),
+            dma((2,)),
             dma((12,)),
         ],
         compiler_params=pltpu.CompilerParams(

time: 30.3 us -> 28.8 us (0.950)
  the two profiles are of different devices: /device:TPU:56 before, /device:TPU:465 now
where the time goes in v4:
time: 28.8 us; the launch traced here: 28.7 us
  Pallas kernels  28 us (97%)
  local copies, waits for them, and re-layouts  0.62 us (2%)
    pallas_call x1, Pallas kernels, local(): pl.pallas_call(kernel, out_shape=jax.ShapeDtypeStruct((16, 1024), BF16),...  28 us
    unnamed x1, local copies, waits for them, and re-layouts  0.62 us

profile of v4, /device:TPU:465, one launch (start us, length us, event | category | flops | bytes accessed | tf_op | source)
XLA Modules:
  0.0 28.7 jit_solution(10366040512267832367)
XLA Ops:
  0.0 28.0 %shard_map.91 = bf16[16,1024]{1,0:T(8,128)(2,1)S(1)} custom-call(bf16[16,1024]{1,0:T(8,128)(2,1)} %vec.1, bf16[1,9,256,256]{3,2,1,0:T(8,128)(2,1)} %blocks.1, s32[1,9]{1,0:T(1,128)} %near_cols.1, s32[1,9]{1,0:T(1,128)} %near_mask.1, bf16[4,32,256]{2,1,0:T(8,128)(2,1)} %basis.1, bf16[6,32,32]{2,1,0:T(8,128)(2,1)} %transfer.1, ...), custom_call_target="tpu_custom_call" | custom-call | tf_op jit(solution)/shard_map/pallas_call | solution.py:598
  28.0 0.6 %copy.11 = bf16[16,1024]{1,0:T(8,128)(2,1)} copy(bf16[16,1024]{1,0:T(8,128)(2,1)S(1)} %shard_map.91) | data formatting | bytes 65536

commit v5 on v4

--- a/solution.py
+++ b/solution.py
@@ -514,9 +514,9 @@
             both = acc_for[half] + pltpu.roll(acc_for[half], 64, 1)
             joint[half] = jnp.where(low, both[0:32], both[32:64])
 
-    lax.fori_loop(own_quad, 2, hear_quad, 0)
-
-    pl.when(late_side)(near_field)
+    lax.fori_loop(own_quad, jnp.where(early, own_quad + 1, own_quad), hear_quad, 0)
+
+    pl.when(late_before)(near_field)
 
     @pl.when(early)
     def _():
@@ -531,6 +531,9 @@
                 device_id_type=MESH,
             ).start()
 
+    pl.when(late_after)(near_field)
+
+    lax.fori_loop(1, jnp.where(own_quad == 0, 2, 1), hear_quad, 0)
     lax.fori_loop(2, QUADS, hear_quad, 0)
     lax.fori_loop(0, own_quad % 2 * early.astype(jnp.int32), hear_quad, 0)
 

time: 28.8 us -> 27.9 us (0.969)
  the two profiles are of different devices: /device:TPU:465 before, /device:TPU:8 now
where the time goes in v5:
time: 27.9 us; the launch traced here: 27.8 us
  Pallas kernels  27.2 us (97%)
  local copies, waits for them, and re-layouts  0.62 us (2%)
    pallas_call x1, Pallas kernels, local(): pl.pallas_call(kernel, out_shape=jax.ShapeDtypeStruct((16, 1024), BF16),...  27.2 us
    unnamed x1, local copies, waits for them, and re-layouts  0.62 us

profile of v5, /device:TPU:8, one launch (start us, length us, event | category | flops | bytes accessed | tf_op | source)
XLA Modules:
  0.0 27.8 jit_solution(12575491426485435560)
XLA Ops:
  0.0 27.2 %shard_map.91 = bf16[16,1024]{1,0:T(8,128)(2,1)S(1)} custom-call(bf16[16,1024]{1,0:T(8,128)(2,1)} %vec.1, bf16[1,9,256,256]{3,2,1,0:T(8,128)(2,1)} %blocks.1, s32[1,9]{1,0:T(1,128)} %near_cols.1, s32[1,9]{1,0:T(1,128)} %near_mask.1, bf16[4,32,256]{2,1,0:T(8,128)(2,1)} %basis.1, bf16[6,32,32]{2,1,0:T(8,128)(2,1)} %transfer.1, ...), custom_call_target="tpu_custom_call" | custom-call | tf_op jit(solution)/shard_map/pallas_call | solution.py:601
  27.2 0.6 %copy.11 = bf16[16,1024]{1,0:T(8,128)(2,1)} copy(bf16[16,1024]{1,0:T(8,128)(2,1)S(1)} %shard_map.91) | data formatting | bytes 65536

commit v6 on v5

--- a/solution.py
+++ b/solution.py
@@ -246,7 +246,7 @@
             odd = jnp.where(low_half, pltpu.roll(a, 64, 1), b)
             slabs[pl.ds(block * 64 + 2 * tile, 8, stride=8), :] = even
             slabs[pl.ds(block * 64 + 2 * tile + 1, 8, stride=8), :] = odd
-    send_v[...] = slabs[...].reshape(128, 8, 128).astype(BF16)
+    send_v[...] = slabs[0:1024].reshape(128, 8, 128).astype(BF16)
 
     near_count = 3 + has(-1).astype(jnp.int32) + has(1).astype(jnp.int32)
     heard = jnp.where(early, (own_quad + 1) * QUAD, group + 1) * MEMBERS - 1
@@ -612,9 +612,9 @@
             vmem((7, 27), jnp.int32),
             vmem((7, 27), jnp.int32),
             vmem((2, 8, 128), F32),
-            vmem((896, 128), F32),
+            vmem((1024, 128), F32),
             vmem((256, 512), BF16),
-            vmem((1024, 128), F32),
+            vmem((1088, 128), F32),
             vmem((128, 8, 128), BF16),
             vmem((128, 1, 32), F32),
             vmem((16, 8, 8, 128), BF16),

time: 27.9 us -> 27.9 us (level)
  no operation moved by 1% of the time
where the time goes in v6:
time: 27.9 us; the launch traced here: 27.8 us
  Pallas kernels  27.2 us (97%)
  local copies, waits for them, and re-layouts  0.62 us (2%)
    pallas_call x1, Pallas kernels, local(): pl.pallas_call(kernel, out_shape=jax.ShapeDtypeStruct((16, 1024), BF16),...  27.2 us
    unnamed x1, local copies, waits for them, and re-layouts  0.62 us

profile of v6, /device:TPU:8, one launch (start us, length us, event | category | flops | bytes accessed | tf_op | source)
XLA Modules:
  0.0 27.8 jit_solution(1763110586130433870)
XLA Ops:
  0.0 27.2 %shard_map.91 = bf16[16,1024]{1,0:T(8,128)(2,1)S(1)} custom-call(bf16[16,1024]{1,0:T(8,128)(2,1)} %vec.1, bf16[1,9,256,256]{3,2,1,0:T(8,128)(2,1)} %blocks.1, s32[1,9]{1,0:T(1,128)} %near_cols.1, s32[1,9]{1,0:T(1,128)} %near_mask.1, bf16[4,32,256]{2,1,0:T(8,128)(2,1)} %basis.1, bf16[6,32,32]{2,1,0:T(8,128)(2,1)} %transfer.1, ...), custom_call_target="tpu_custom_call" | custom-call | tf_op jit(solution)/shard_map/pallas_call | solution.py:601
  27.2 0.6 %copy.11 = bf16[16,1024]{1,0:T(8,128)(2,1)} copy(bf16[16,1024]{1,0:T(8,128)(2,1)S(1)} %shard_map.91) | data formatting | bytes 65536
